TPU v7x, 8 devices: a whole 2x2x1 slice. The times are simulated.
8 devices in a mesh: dp: 8 (over z, y, x, core).
Axes of the slice: x: 2, y: 2, z: 1, core: 2. Of those that a mesh axis runs over, the one named last changes fastest.
Arguments:
- act_in: bfloat16 [2048, 7, 7, 512], P('dp')
- shortcut: bfloat16 [2048, 7, 7, 2048], P('dp')
- labels: int32 [2048], P('dp')
- w_conv: float32 [512, 2048], replicated
- bn_gamma: float32 [2048], replicated
- bn_beta: float32 [2048], replicated
- w_fc: float32 [2048, 21843], replicated
- fc_bias: float32 [21843], replicated
- vel_conv: float32 [512, 2048], replicated
- vel_gamma: float32 [2048], replicated
- vel_beta: float32 [2048], replicated
- vel_fc: float32 [2048, 21843], replicated
- vel_bias: float32 [21843], replicated
- learn_rate: float32 [], replicated
Outputs:
- output 1: float32 [512, 2048], replicated
- output 2: float32 [2048], replicated
- output 3: float32 [2048], replicated
- output 4: float32 [2048, 21843], replicated
- output 5: float32 [21843], replicated
- output 6: float32 [512, 2048], replicated
- output 7: float32 [2048], replicated
- output 8: float32 [2048], replicated
- output 9: float32 [2048, 21843], replicated
- output 10: float32 [21843], replicated
- output 11: float32 [], replicated
All inputs are finite; a program needn't handle non-finite values.
Results may differ from a plain program's by a relative error of at most 0.00856896.
Values sent between devices are 32-bit elements.
A program may use at most 3 GiB of HBM per device.

v0:
```python
import jax
import jax.numpy as jnp
from jax import lax
from jax.sharding import PartitionSpec as P

BN_EPS = 1e-5
SMOOTHING = 0.1
MOMENTUM = 0.9
TRUST_COEF = 0.001
WEIGHT_DECAY = 5e-5


def forward_backward(act_in, shortcut, labels, w_conv, bn_gamma, bn_beta, w_fc, fc_bias, global_rows):
    per_dev = act_in.shape[0]
    spatial = act_in.shape[1] * act_in.shape[2]
    c_mid = act_in.shape[3]
    c_out = shortcut.shape[3]
    classes = w_fc.shape[1]
    pos_count = per_dev * spatial
    act_grid = act_in.reshape(per_dev, spatial, c_mid)
    conv_out = jnp.einsum('bpc,cd->bpd', act_grid, w_conv.astype(jnp.bfloat16), preferred_element_type=jnp.float32)
    batch_mean = jnp.mean(conv_out, axis=(0, 1))
    centered = conv_out - batch_mean
    inv_std = lax.rsqrt(jnp.mean(jnp.square(centered), axis=(0, 1)) + BN_EPS)
    x_hat = centered * inv_std
    pre_act = x_hat * bn_gamma + bn_beta + shortcut.reshape(per_dev, spatial, c_out).astype(jnp.float32)
    pooled = jnp.mean(jax.nn.relu(pre_act), axis=1)
    pooled_bf = pooled.astype(jnp.bfloat16)
    fc_bf = w_fc.astype(jnp.bfloat16)
    logits = jnp.dot(pooled_bf, fc_bf, preferred_element_type=jnp.float32) + fc_bias
    log_prob = jax.nn.log_softmax(logits, axis=-1)
    one_hot_lab = (labels[:, None] == jnp.arange(classes, dtype=jnp.int32)[None, :]).astype(jnp.float32)
    target = SMOOTHING / classes + (1.0 - SMOOTHING) * one_hot_lab
    loss_part = -jnp.sum(target * log_prob) / global_rows
    d_logits = (jnp.exp(log_prob) - target) / global_rows
    d_bias = jnp.sum(d_logits, axis=0)
    d_logits_bf = d_logits.astype(jnp.bfloat16)
    d_fc = jnp.einsum('bc,bk->ck', pooled_bf, d_logits_bf, preferred_element_type=jnp.float32)
    d_pool = jnp.einsum('bk,ck->bc', d_logits_bf, fc_bf, preferred_element_type=jnp.float32) / spatial
    d_pre = jnp.where(pre_act > 0, d_pool[:, None, :], 0.0)
    d_beta = jnp.sum(d_pre, axis=(0, 1))
    d_gamma = jnp.sum(d_pre * x_hat, axis=(0, 1))
    d_conv_out = (bn_gamma * inv_std) * (d_pre - d_beta / pos_count - x_hat * (d_gamma / pos_count))
    d_conv = jnp.einsum('bpc,bpd->cd', act_grid, d_conv_out.astype(jnp.bfloat16), preferred_element_type=jnp.float32)
    return d_conv, d_gamma, d_beta, d_fc, d_bias, loss_part


def lars_update(weight, gradient, velocity, learn_rate):
    w_norm = jnp.sqrt(jnp.sum(jnp.square(weight)))
    g_norm = jnp.sqrt(jnp.sum(jnp.square(gradient)))
    trust = TRUST_COEF * w_norm / (g_norm + WEIGHT_DECAY * w_norm)
    new_vel = MOMENTUM * velocity + learn_rate * trust * (gradient + WEIGHT_DECAY * weight)
    return weight - new_vel, new_vel


def solution(mesh):
    groups = mesh.shape['dp']

    def local_step(act_in, shortcut, labels, w_conv, bn_gamma, bn_beta, w_fc, fc_bias, vel_conv, vel_gamma, vel_beta, vel_fc, vel_bias, learn_rate):
        global_rows = act_in.shape[0] * groups
        local_terms = forward_backward(act_in, shortcut, labels, w_conv, bn_gamma, bn_beta, w_fc, fc_bias, global_rows)
        g_conv, g_gamma, g_beta, g_fc, g_bias, loss_val = lax.psum(local_terms, 'dp')
        conv_new, conv_vel_new = lars_update(w_conv, g_conv, vel_conv, learn_rate)
        fc_new, fc_vel_new = lars_update(w_fc, g_fc, vel_fc, learn_rate)
        gamma_vel_new = MOMENTUM * vel_gamma + learn_rate * g_gamma
        beta_vel_new = MOMENTUM * vel_beta + learn_rate * g_beta
        bias_vel_new = MOMENTUM * vel_bias + learn_rate * g_bias
        return (conv_new, bn_gamma - gamma_vel_new, bn_beta - beta_vel_new, fc_new, fc_bias - bias_vel_new, conv_vel_new, gamma_vel_new, beta_vel_new, fc_vel_new, bias_vel_new, loss_val)

    return jax.shard_map(local_step, mesh=mesh, in_specs=(P('dp'),) * 3 + (P(),) * 11, out_specs=(P(),) * 11, check_vma=False)
```

profile of v0, /device:TPU:0, one launch (start us, length us, event | category | flops | bytes accessed | tf_op | source)
XLA Modules:
  0.0 2801.7 jit_solution(16138456963969682893)
XLA Ops:
  7.2 0.0 all-reduce.7.cloned.1.call-start
  7.2 43.4 %fusion.36 = (f32[2048]{0:T(1024)S(1)}, f32[256,49,2048]{2,0,1:T(8,128)}) fusion(bf16[256,49,512]{2,0,1:T(8,128)(2,1)} %bitcast.20, f32[512,2048]{1,0:T(8,128)} %param.17), kind=kOutput, calls=%fused_computation.54 | convolution fusion | flops 26333411328 | bytes 119808000 | tf_op jit(solution)/shard_map/bpc,cd->bpd/dot_general | solution.py:21
  50.7 0.0 copy-start.7
  50.7 0.0 copy-start.8
  50.7 31.1 %multiply_reduce_fusion.2 = f32[2048]{0:T(1024)S(1)} fusion(f32[256,49,2048]{2,0,1:T(8,128)} %get-tuple-element.44, f32[2048]{0:T(1024)S(1)} %broadcast_multiply_fusion.2), kind=kLoop, calls=%fused_computation.12 | loop fusion | flops 77068288 | bytes 102776832 | tf_op jit(solution)/shard_map/reduce_sum | solution.py:24
  81.8 0.0 copy-start.10
  81.8 0.6 copy-done.10
  82.4 0.0 copy-done.7
  82.4 0.0 copy-done.8
  82.4 0.0 copy-start.3
  82.4 47.0 %maximum_reduce_fusion = f32[256,2048]{1,0:T(8,128)S(1)} fusion(bf16[256,7,7,2048]{3,0,2,1:T(8,128)(2,1)} %param.15, f32[2048]{0:T(1024)S(1)} %copy-done.8, f32[2048]{0:T(1024)S(1)} %copy-done.7, f32[2048]{0:T(1024)S(1)} %add_rsqrt_fusion, f32[256,49,2048]{2,0,1:T(8,128)} %get-tuple-element.44, f32[2048]{0:T(1024)S(1)} %broadcast_multiply_fusion.2), kind=kLoop, calls=%fused_computation.11 | loop fusion | flops 204996608 | bytes 156270592 | tf_op jit(solution)/shard_map/reduce_sum | solution.py:27
  129.4 0.0 copy-done.3
  129.4 0.0 copy-start
  129.4 70.7 %fusion.37 = (f32[256]{0:T(256)S(1)}, f32[256,21843]{0,1:T(8,128)}) fusion(f32[21843]{0:T(1024)S(1)} %copy-done.3, f32[2048,21843]{0,1:T(8,128)} %param.20, f32[256,2048]{1,0:T(8,128)S(1)} %maximum_reduce_fusion), kind=kOutput, calls=%fused_computation.55 | convolution fusion | flops 22961010688 | bytes 203490640 | tf_op jit(solution)/shard_map/dot_general | solution.py:30
  200.1 0.0 copy-done
  200.1 0.0 copy-start.12
  200.1 9.2 exponential_reduce_fusion
  209.3 0.0 copy-done.12
  209.3 63.0 %fusion.18 = f32[256,2048]{1,0:T(8,128)S(1)} fusion(f32[2048,21843]{0,1:T(8,128)} %param.20, f32[256,21843]{0,1:T(8,128)} %get-tuple-element.46, s32[256]{0:T(256)S(1)} %copy-done.12, f32[256]{0:T(256)S(1)} %log.9, f32[256]{0:T(256)S(1)} %get-tuple-element.45), kind=kOutput, calls=%fused_computation.32 | convolution fusion | flops 22994038784 | bytes 203405312 | tf_op jit(solution)/shard_map/bk,ck->bc/dot_general | solution.py:39
  272.3 0.0 copy-start.2
  272.4 14.7 multiply_reduce_fusion.3
  287.1 0.0 copy-start.11
  287.1 0.0 copy-start.13
  287.1 57.7 %select_reduce_fusion = (f32[2048]{0:T(1024)S(1)}, f32[2048]{0:T(1024)S(1)}, pred[256,49,2048]{2,0,1:T(32,128)(4,1)}) fusion(f32[256,2048]{1,0:T(8,128)S(1)} %fusion.18, f32[2048]{0:T(1024)S(1)} %add_rsqrt_fusion, f32[256,49,2048]{2,0,1:T(8,128)} %get-tuple-element.44, f32[2048]{0:T(1024)S(1)} %broadcast_multiply_fusion.2, ...), kind=kLoop, calls=%fused_computation.5 | loop fusion | flops 282587136 | bytes 181977088 | tf_op jit(solution)/shard_map/reduce_sum | solution.py:41
  344.8 0.0 copy-done.2
  345.5 25.5 all-reduce
  371.7 0.0 copy-done.11
  371.7 0.0 copy-done.13
  371.7 0.6 fusion.34
  372.3 0.0 copy-start.1
  372.3 52.7 %fusion.15 = f32[512,2048]{0,1:T(8,128)} fusion(bf16[256,49,512]{2,0,1:T(8,128)(2,1)} %bitcast.21, pred[256,49,2048]{2,0,1:T(32,128)(4,1)} %get-tuple-element.41, f32[256,49,2048]{2,0,1:T(8,128)} %get-tuple-element.44, f32[2048]{0:T(1024)S(1)} %get-tuple-element.47, f32[2048]{0:T(1024)S(1)} %get-tuple-element.48, f32[256,2048]{1,0:T(8,128)} %copy-done.2, ...), kind=kOutput, calls=%fused_computation.31 | convolution fusion | flops 26512195584 | bytes 147628032 | tf_op jit(solution)/shard_map/bpc,bpd->cd/dot_general | solution.py:44
  425.0 0.0 all-reduce.7.cloned.1.call-update
  425.0 0.0 all-reduce.5.cloned.1.call-start
  425.1 0.0 copy-done.1
  425.1 66.8 %fusion.24 = f32[2048,21843]{0,1:T(8,128)} fusion(f32[256,2048]{1,0:T(8,128)S(1)} %copy-done.1, f32[256,21843]{0,1:T(8,128)} %get-tuple-element.46, s32[256]{0:T(256)S(1)} %copy-done.12, f32[256]{0:T(256)S(1)} %log.9, f32[256]{0:T(256)S(1)} %get-tuple-element.45), kind=kOutput, calls=%fused_computation.37 | convolution fusion | flops 22949828608 | bytes 203405312 | tf_op jit(solution)/shard_map/bc,bk->ck/dot_general | solution.py:38
  491.9 0.0 all-reduce.5.cloned.1.call-update
  492.0 5.3 copy.28
  497.3 3.9 multiply_reduce_fusion.5
  501.9 0.0 copy-start.9
  501.9 0.0 copy-start.14
  501.9 0.0 copy-start.15
  501.9 55.5 %multiply_reduce_fusion.1 = f32[]{:T(128)} fusion(f32[2048,21843]{0,1:T(8,128)} %param.20), kind=kLoop, calls=%fused_computation.2 | loop fusion | flops 89468928 | bytes 178937856 | tf_op jit(solution)/shard_map/reduce_sum | solution.py:49
  558.1 5.3 copy.25
  563.4 0.0 copy-start.4
  563.4 0.0 copy-start.5
  563.4 0.0 copy-done.9
  563.4 0.0 copy-done.14
  563.5 0.0 copy-done.15
  563.5 0.6 fusion.33
  564.1 0.0 all-reduce.7.cloned.1.call-done
  564.1 0.0 copy-start.6
  564.1 3.9 multiply_reduce_fusion.4
  568.7 9.7 fusion.35
  578.4 5.3 copy.29
  583.7 5.3 copy.30
  589.1 0.0 copy-done.4
  589.1 0.0 copy-done.5
  589.1 0.0 copy-done.6
  589.1 0.7 fusion.31
  589.8 1862.3 %all-reduce.5.cloned.1.call-done = f32[2048,21843]{0,1:T(8,128)} async-done(((f32[2048,21843]{0,1:T(8,128)}), f32[2048,21843]{0,1:T(8,128)}) %all-reduce.5.cloned.1.call-update) | async-done | bytes 178937872 | tf_op jit(solution)/shard_map/psum | solution.py:62
  2452.1 55.4 %multiply_reduce_fusion = f32[]{:T(128)} fusion(f32[2048,21843]{0,1:T(8,128)} %all-reduce.5.cloned.1.call-done), kind=kLoop, calls=%fused_computation.1 | loop fusion | flops 89468928 | bytes 178937856 | tf_op jit(solution)/shard_map/reduce_sum | solution.py:50
  2508.2 286.2 %fusion.32 = (f32[2048,21843]{0,1:T(8,128)}, f32[2048,21843]{0,1:T(8,128)}) fusion(f32[2048,21843]{0,1:T(8,128)} %param.20, f32[2048,21843]{0,1:T(8,128)} %all-reduce.5.cloned.1.call-done, f32[]{:T(128)S(6)} %mul.159, f32[2048,21843]{0,1:T(8,128)} %param.25), kind=kLoop, calls=%fused_computation.50 | loop fusion | flops 268406784 | bytes 894689280 | tf_op jit(solution)/shard_map/sub | solution.py:53
  (4 shorter events, 0.0 us)
Async XLA Ops:
  7.2 556.9 %all-reduce.7.cloned.1.call-start = ((), (), s32[]{:S(2)}) async-start(), calls=%async_computation.1 | async-start | bytes 8568832 | tf_op jit(solution)/shard_map/psum | solution.py:62
  50.7 31.7 %copy-start.7 = (f32[2048]{0:T(1024)S(1)}, f32[2048]{0:T(1024)}, u32[]{:S(2)}) copy-start(f32[2048]{0:T(1024)} %param.18) | copy-start | bytes 24580
  50.7 31.7 %copy-start.8 = (f32[2048]{0:T(1024)S(1)}, f32[2048]{0:T(1024)}, u32[]{:S(2)}) copy-start(f32[2048]{0:T(1024)} %param.19) | copy-start | bytes 24580
  81.8 0.6 copy-start.10
  82.4 47.0 %copy-start.3 = (f32[21843]{0:T(1024)S(1)}, f32[21843]{0:T(1024)}, u32[]{:S(2)}) copy-start(f32[21843]{0:T(1024)} %param.21) | copy-start | bytes 262120
  129.4 70.7 %copy-start = (f32[256,2048]{1,0:T(8,128)}, f32[256,2048]{1,0:T(8,128)S(1)}, u32[]{:S(2)}) copy-start(f32[256,2048]{1,0:T(8,128)S(1)} %maximum_reduce_fusion) | copy-start | bytes 6291460
  200.1 9.2 copy-start.12
  272.3 72.5 %copy-start.2 = (f32[256,2048]{1,0:T(8,128)}, f32[256,2048]{1,0:T(8,128)S(1)}, u32[]{:S(2)}) copy-start(f32[256,2048]{1,0:T(8,128)S(1)} %fusion.18) | copy-start | bytes 6291460
  287.1 84.6 %copy-start.11 = (f32[2048]{0:T(1024)S(1)}, f32[2048]{0:T(1024)}, u32[]{:S(2)}) copy-start(f32[2048]{0:T(1024)} %copy-done.10) | copy-start | bytes 24580
  287.1 84.6 %copy-start.13 = (f32[2048]{0:T(1024)S(1)}, f32[2048]{0:T(1024)}, u32[]{:S(2)}) copy-start(f32[2048]{0:T(1024)} %param.23) | copy-start | bytes 24580
  372.3 52.8 %copy-start.1 = (f32[256,2048]{1,0:T(8,128)S(1)}, f32[256,2048]{1,0:T(8,128)}, u32[]{:S(2)}) copy-start(f32[256,2048]{1,0:T(8,128)} %copy-done) | copy-start | bytes 6291460
  425.0 2027.1 %all-reduce.5.cloned.1.call-start = ((), (), s32[]{:S(2)}) async-start(), calls=%async_computation | async-start | bytes 357957632 | tf_op jit(solution)/shard_map/psum | solution.py:62
  501.9 61.6 %copy-start.9 = (f32[2048]{0:T(1024)S(1)}, f32[2048]{0:T(1024)}, u32[]{:S(2)}) copy-start(f32[2048]{0:T(1024)} %param.19) | copy-start | bytes 24580
  501.9 61.6 %copy-start.14 = (f32[2048]{0:T(1024)S(1)}, f32[2048]{0:T(1024)}, u32[]{:S(2)}) copy-start(f32[2048]{0:T(1024)} %param.24) | copy-start | bytes 24580
  501.9 61.5 %copy-start.15 = (f32[2048]{0:T(1024)S(1)}, f32[2048]{0:T(1024)}, u32[]{:S(2)}) copy-start(f32[2048]{0:T(1024)} %get-tuple-element.27) | copy-start | bytes 24580
  563.4 25.6 copy-start.4
  563.4 25.6 copy-start.5
  564.1 25.0 copy-start.6
Sparse Core Ops, SparseCore 0:
  425.2 71.8 all-reduce.6
  501.4 1950.6 all-reduce.4
where the time goes:
time: 2810 us; the launch traced here: 2800 us
  waiting for transfers between devices  1860 us (66%)
  other arithmetic  576 us (20%)
  matrix products  297 us (11%)
    psum x2, waiting for transfers between devices, local_step(): lax.psum(local_terms, 'dp')  1860 us
    sub x2, other arithmetic, lars_update(): return (weight - new_vel, new_vel)  296 us
    dot_general x1, matrix products, forward_backward(): jnp.dot(pooled_bf, fc_bf, preferred_element_type=jnp.float32) + fc_bias  70.7 us
    dot_general x1, matrix products, forward_backward(): jnp.einsum('bc,bk->ck', pooled_bf, d_logits_bf, preferred_element_type=jn...  66.8 us
    dot_general x1, matrix products, forward_backward(): jnp.einsum('bk,ck->bc', d_logits_bf, fc_bf, preferred_element_type=jnp.fl...  63 us
    reduce_sum x2, other arithmetic, lars_update(): w_norm = jnp.sqrt(jnp.sum(jnp.square(weight)))  59.3 us
    reduce_sum x2, other arithmetic, lars_update(): g_norm = jnp.sqrt(jnp.sum(jnp.square(gradient)))  59.3 us
    reduce_sum x1, other arithmetic, forward_backward(): d_beta = jnp.sum(d_pre, axis=(0, 1))  57.7 us
  transfers between devices with their start and end apart: 2, of which 1 were waited for; matrix products, arithmetic and copies ran while one was open for 6% of the time, Pallas kernels for 0%

commit v1 on v0

v1 whole, which is shorter than its diff:
```python
import functools

import jax
import jax.numpy as jnp
from jax import lax
from jax.experimental import pallas as pl
from jax.experimental.pallas import tpu as pltpu
from jax.sharding import PartitionSpec as P

BN_EPS = 1e-5
SMOOTHING = 0.1
MOMENTUM = 0.9
TRUST_COEF = 0.001
WEIGHT_DECAY = 5e-5

TILE = 256
BLK = 32
SLOTS = TILE // BLK
HAVE = 3
NORM = 2
GROUP = 3
CHUNK = 512
VMEM_LIMIT = 66_000_000


def tiled(x, reps):
    return jnp.concatenate([x] * reps, axis=1)


def logit_grads(z, bias, lse, lab, base, classes):
    cols = z.shape[1]
    row = lax.broadcasted_iota(jnp.int32, (BLK, cols), 0) + base
    e = jnp.exp(z + tiled(bias, cols // 128) - lse)
    low = SMOOTHING / classes
    return e - jnp.where(lab == row, low + (1.0 - SMOOTHING), low)


def grad_kernel(classes, rows_total, sc, *refs):
    nw = GROUP * HAVE
    ws, biases = refs[:nw], refs[nw:nw + GROUP]
    pt, p, lse, lab, g_out, db_out, sq_out, lhs, dmat = refs[nw + GROUP:]
    q, c = sc[0], sc[1]
    step = pl.program_id(0)
    cols = pt.shape[1]
    feats = pt.shape[0]

    @pl.when(step == 0)
    def _():
        sq_out[...] = jnp.zeros_like(sq_out)

    bases, slots = [], []
    for t in range(GROUP):
        tile = 2 * (GROUP * step + t) + c
        for i in range(HAVE):
            slot = lax.rem(2 * q + i, SLOTS)
            slots.append(slot)
            bases.append(tile * TILE + slot * BLK)
    for k in range(nw):
        valid = lax.broadcasted_iota(jnp.int32, (BLK, feats), 0) < classes - bases[k]
        w = jnp.where(valid, ws[k][...], 0.0)
        if k % HAVE < NORM:
            sq_out[1] += jnp.sum((w * w).reshape(BLK // 8, 8, feats), axis=0)
        lhs[k * BLK:(k + 1) * BLK, :] = w.astype(jnp.bfloat16)
    sums = [jnp.zeros((BLK, 128), jnp.float32) for _ in range(nw)]
    for n in range(cols // CHUNK):
        cs = slice(n * CHUNK, (n + 1) * CHUNK)
        z = jnp.dot(lhs[...], pt[:, cs], preferred_element_type=jnp.float32)
        for k in range(nw):
            rs = slice(k * BLK, (k + 1) * BLK)
            bias = biases[k // HAVE][pl.ds(pl.multiple_of(slots[k] * BLK, BLK), BLK), :]
            d = logit_grads(z[rs], bias, lse[:, cs], lab[:, cs], bases[k], classes)
            valid = lax.broadcasted_iota(jnp.int32, (BLK, CHUNK), 0) < classes - bases[k]
            d = jnp.where(valid, d, 0.0)
            for m in range(CHUNK // 128):
                sums[k] = sums[k] + d[:, m * 128:(m + 1) * 128]
            dmat[rs, cs] = d.astype(jnp.bfloat16)
    for k in range(nw):
        db_out[k // HAVE, (k % HAVE) * BLK:(k % HAVE + 1) * BLK, :] = sums[k]
    for n in range(feats // CHUNK):
        cs = slice(n * CHUNK, (n + 1) * CHUNK)
        g = jnp.dot(dmat[...], p[:, cs], preferred_element_type=jnp.float32) * (1.0 / rows_total)
        for k in range(nw):
            gk = g[k * BLK:(k + 1) * BLK]
            g_out[k // HAVE, (k % HAVE) * BLK:(k % HAVE + 1) * BLK, cs] = gk
            if k % HAVE < NORM:
                sq_out[0, :, cs] += jnp.sum((gk * gk).reshape(BLK // 8, 8, CHUNK), axis=0)


def shared_grads(sc, wt, bias, pt, p, lse, lab):
    classes, feats = wt.shape
    rows_total = p.shape[0]
    n_tiles = pl.cdiv(classes, TILE)
    steps = pl.cdiv(pl.cdiv(n_tiles, 2), GROUP)
    last = pl.cdiv(classes, BLK) - 1

    def w_map(t, i):
        return lambda s, sc: (jnp.minimum((2 * (GROUP * s + t) + sc[1]) * SLOTS + lax.rem(2 * sc[0] + i, SLOTS), last), 0)

    def b_map(t):
        return lambda s, sc: (jnp.minimum(2 * (GROUP * s + t) + sc[1], n_tiles - 1), 0)

    once = dict(pipeline_mode=pl.Buffered(1))
    whole = lambda a: pl.BlockSpec(a.shape, lambda s, sc: (0, 0), **once)
    rows = GROUP * HAVE * BLK
    return pl.pallas_call(
        functools.partial(grad_kernel, classes, rows_total),
        grid_spec=pltpu.PrefetchScalarGridSpec(
            num_scalar_prefetch=1,
            grid=(steps,),
            in_specs=[pl.BlockSpec((BLK, feats), w_map(t, i)) for t in range(GROUP) for i in range(HAVE)]
            + [pl.BlockSpec((TILE, 128), b_map(t)) for t in range(GROUP)]
            + [whole(pt), whole(p), whole(lse), whole(lab)],
            out_specs=[
                pl.BlockSpec((GROUP, HAVE * BLK, feats), lambda s, sc: (s, 0, 0)),
                pl.BlockSpec((GROUP, HAVE * BLK, 128), lambda s, sc: (s, 0, 0)),
                pl.BlockSpec((2, 8, feats), lambda s, sc: (0, 0, 0)),
            ],
            scratch_shapes=[pltpu.VMEM((rows, feats), jnp.bfloat16), pltpu.VMEM((rows, rows_total), jnp.bfloat16)],
        ),
        out_shape=[
            jax.ShapeDtypeStruct((steps * GROUP, HAVE * BLK, feats), jnp.float32),
            jax.ShapeDtypeStruct((steps * GROUP, HAVE * BLK, 128), jnp.float32),
            jax.ShapeDtypeStruct((2, 8, feats), jnp.float32),
        ],
        compiler_params=pltpu.CompilerParams(dimension_semantics=("arbitrary",), vmem_limit_bytes=VMEM_LIMIT),
        cost_estimate=pl.CostEstimate(flops=4 * steps * rows * feats * rows_total, bytes_accessed=8 * steps * rows * feats, transcendentals=0),
        name="shared_grads",
    )(sc, *([wt] * (GROUP * HAVE)), *([bias] * GROUP), pt, p, lse, lab)


def update_kernel(classes, rows_total, sc, rate, w_in, v_in, own, other, bias, pt, p, lse, lab, w_out, v_out, lhs, dmat):
    q, c = sc[0], sc[1]
    step = pl.program_id(0)
    a = rate[0]
    cols = pt.shape[1]
    feats = pt.shape[0]

    def rows_at(base):
        return pl.ds(pl.multiple_of(base, BLK), BLK)

    def apply(rs, cs, g):
        w = w_in[rs, cs]
        nv = MOMENTUM * v_in[rs, cs] + a * (g + WEIGHT_DECAY * w)
        v_out[rs, cs] = nv
        w_out[rs, cs] = w - nv

    bases = []
    for t in range(2):
        for i in range(HAVE, SLOTS):
            bases.append(t * TILE + lax.rem(2 * q + i, SLOTS) * BLK)
    for k, base in enumerate(bases):
        lhs[k * BLK:(k + 1) * BLK, :] = w_in[rows_at(base), :].astype(jnp.bfloat16)
    known = []
    for src, t in ((own, c), (other, 1 - c)):
        for i in range(HAVE):
            known.append((src, i, t * TILE + lax.rem(2 * q + i, SLOTS) * BLK))
    for n in range(cols // CHUNK):
        cs = slice(n * CHUNK, (n + 1) * CHUNK)
        z = jnp.dot(lhs[...], pt[:, cs], preferred_element_type=jnp.float32)
        for src, i, base in known:
            apply(rows_at(base), cs, src[0, i * BLK:(i + 1) * BLK, cs])
        for k, base in enumerate(bases):
            rs = slice(k * BLK, (k + 1) * BLK)
            d = logit_grads(z[rs], bias[rows_at(base), :], lse[:, cs], lab[:, cs], step * 2 * TILE + base, classes)
            dmat[rs, cs] = d.astype(jnp.bfloat16)
    for n in range(feats // CHUNK):
        cs = slice(n * CHUNK, (n + 1) * CHUNK)
        g = jnp.dot(dmat[...], p[:, cs], preferred_element_type=jnp.float32) * (1.0 / rows_total)
        for k, base in enumerate(bases):
            apply(rows_at(base), cs, g[k * BLK:(k + 1) * BLK])


def fused_update(sc, rate, wt, vt, own, other, bias, pt, p, lse, lab):
    classes, feats = wt.shape
    rows_total = p.shape[0]
    steps = pl.cdiv(classes, 2 * TILE)
    once = dict(pipeline_mode=pl.Buffered(1))
    whole = lambda a: pl.BlockSpec(a.shape, lambda s, sc: (0, 0), **once)
    tile = pl.BlockSpec((2 * TILE, feats), lambda s, sc: (s, 0))
    part = pl.BlockSpec((1, HAVE * BLK, feats), lambda s, sc: (s, 0, 0))
    rows = 2 * (SLOTS - HAVE) * BLK
    return pl.pallas_call(
        functools.partial(update_kernel, classes, rows_total),
        grid_spec=pltpu.PrefetchScalarGridSpec(
            num_scalar_prefetch=1,
            grid=(steps,),
            in_specs=[pl.BlockSpec(memory_space=pltpu.SMEM), tile, tile, part, part,
                      pl.BlockSpec((2 * TILE, 128), lambda s, sc: (s, 0)),
                      whole(pt), whole(p), whole(lse), whole(lab)],
            out_specs=[tile, tile],
            scratch_shapes=[pltpu.VMEM((rows, feats), jnp.bfloat16), pltpu.VMEM((rows, rows_total), jnp.bfloat16)],
        ),
        out_shape=[jax.ShapeDtypeStruct(wt.shape, jnp.float32)] * 2,
        compiler_params=pltpu.CompilerParams(dimension_semantics=("arbitrary",), vmem_limit_bytes=VMEM_LIMIT),
        cost_estimate=pl.CostEstimate(flops=4 * steps * rows * feats * rows_total, bytes_accessed=16 * classes * feats, transcendentals=0),
        name="fused_update",
    )(sc, rate, wt, vt, own, other, bias, pt, p, lse, lab)


def round_kernel(x, p, pt):
    r = x[...].astype(jnp.bfloat16)
    p[...] = r
    pt[...] = r.T


def round_both(x):
    n, m = x.shape
    return pl.pallas_call(
        round_kernel,
        grid=(n // TILE,),
        in_specs=[pl.BlockSpec((TILE, m), lambda i: (i, 0))],
        out_specs=[pl.BlockSpec((TILE, m), lambda i: (i, 0)), pl.BlockSpec((m, TILE), lambda i: (0, i))],
        out_shape=[jax.ShapeDtypeStruct((n, m), jnp.bfloat16), jax.ShapeDtypeStruct((m, n), jnp.bfloat16)],
        compiler_params=pltpu.CompilerParams(dimension_semantics=("arbitrary",)),
        cost_estimate=pl.CostEstimate(flops=2 * n * m, bytes_accessed=8 * n * m, transcendentals=0),
        name="round_both",
    )(x)


def solution(mesh):
    groups = mesh.shape['dp']
    swap = [(i, i ^ 1) for i in range(groups)]

    def local_step(act_in, shortcut, labels, w_conv, bn_gamma, bn_beta, w_fc, fc_bias, vel_conv, vel_gamma, vel_beta, vel_fc, vel_bias, learn_rate):
        per_dev = act_in.shape[0]
        global_rows = per_dev * groups
        spatial = act_in.shape[1] * act_in.shape[2]
        c_mid = act_in.shape[3]
        c_out = shortcut.shape[3]
        classes = w_fc.shape[1]
        pos_count = per_dev * spatial
        dev = lax.axis_index('dp')
        sc = jnp.stack([dev // 2, dev % 2]).astype(jnp.int32)
        act_grid = act_in.reshape(per_dev, spatial, c_mid)
        conv_out = jnp.einsum('bpc,cd->bpd', act_grid, w_conv.astype(jnp.bfloat16), preferred_element_type=jnp.float32)
        batch_mean = jnp.mean(conv_out, axis=(0, 1))
        centered = conv_out - batch_mean
        inv_std = lax.rsqrt(jnp.mean(jnp.square(centered), axis=(0, 1)) + BN_EPS)
        x_hat = centered * inv_std
        pre_act = x_hat * bn_gamma + bn_beta + shortcut.reshape(per_dev, spatial, c_out).astype(jnp.float32)
        pooled = jnp.mean(jax.nn.relu(pre_act), axis=1)
        pooled_bf = pooled.astype(jnp.bfloat16)
        p_all = lax.all_gather(pooled, 'dp', tiled=True)
        fc_bf = w_fc.astype(jnp.bfloat16)
        logits = jnp.dot(pooled_bf, fc_bf, preferred_element_type=jnp.float32) + fc_bias
        top = jnp.max(logits, axis=-1, keepdims=True)
        lse = top + jnp.log(jnp.sum(jnp.exp(logits - top), axis=-1, keepdims=True))
        one_hot_lab = (labels[:, None] == jnp.arange(classes, dtype=jnp.int32)[None, :]).astype(jnp.float32)
        target = SMOOTHING / classes + (1.0 - SMOOTHING) * one_hot_lab
        log_prob = logits - lse
        loss_part = -jnp.sum(target * log_prob) / global_rows
        d_logits_bf = (jnp.exp(log_prob) - target).astype(jnp.bfloat16)
        d_pool = jnp.einsum('bk,ck->bc', d_logits_bf, fc_bf, preferred_element_type=jnp.float32) / (spatial * global_rows)
        d_pre = jnp.where(pre_act > 0, d_pool[:, None, :], 0.0)
        d_beta = jnp.sum(d_pre, axis=(0, 1))
        d_gamma = jnp.sum(d_pre * x_hat, axis=(0, 1))
        d_conv_out = (bn_gamma * inv_std) * (d_pre - d_beta / pos_count - x_hat * (d_gamma / pos_count))
        d_conv = jnp.einsum('bpc,bpd->cd', act_grid, d_conv_out.astype(jnp.bfloat16), preferred_element_type=jnp.float32)

        small = lax.all_gather(jnp.concatenate([lse, labels[:, None].astype(jnp.float32)], axis=1), 'dp', tiled=True)
        lse_all = small[:, 0][None, :]
        lab_all = small[:, 1].astype(jnp.int32)[None, :]
        p_bf, pt_bf = round_both(p_all)
        wt, vt = w_fc.T, vel_fc.T
        n_tiles = pl.cdiv(classes, TILE)
        bias_wide = jnp.broadcast_to(jnp.pad(fc_bias, (0, n_tiles * TILE - classes))[:, None], (n_tiles * TILE, 128))
        own, db, sq = shared_grads(sc, wt, bias_wide, pt_bf, p_bf, lse_all, lab_all)
        other = lax.ppermute(own, 'dp', swap)
        sq = jnp.sum(sq, axis=(1, 2))
        half = pl.cdiv(n_tiles, 2)
        db = jnp.sum(db[:half, :NORM * BLK], axis=-1) / global_rows
        d_bias = lax.dynamic_update_slice(jnp.zeros((half, 2, TILE), jnp.float32), db[:, None, :], (0, sc[1], sc[0] * NORM * BLK))
        d_bias = d_bias.reshape(-1)[:classes]
        sq, g_gamma, g_beta, loss_val = lax.psum((sq, d_gamma, d_beta, loss_part), 'dp')
        g_conv, g_bias = lax.psum((d_conv, d_bias), 'dp')
        g_norm, w_norm = jnp.sqrt(sq[0]), jnp.sqrt(sq[1])
        rate = learn_rate * TRUST_COEF * w_norm / (g_norm + WEIGHT_DECAY * w_norm)
        fc_new, fc_vel_new = fused_update(sc, rate[None], wt, vt, own, other, bias_wide, pt_bf, p_bf, lse_all, lab_all)
        cw = jnp.sqrt(jnp.sum(jnp.square(w_conv)))
        cg = jnp.sqrt(jnp.sum(jnp.square(g_conv)))
        trust = TRUST_COEF * cw / (cg + WEIGHT_DECAY * cw)
        conv_vel_new = MOMENTUM * vel_conv + learn_rate * trust * (g_conv + WEIGHT_DECAY * w_conv)
        gamma_vel_new = MOMENTUM * vel_gamma + learn_rate * g_gamma
        beta_vel_new = MOMENTUM * vel_beta + learn_rate * g_beta
        bias_vel_new = MOMENTUM * vel_bias + learn_rate * g_bias
        return (w_conv - conv_vel_new, bn_gamma - gamma_vel_new, bn_beta - beta_vel_new, fc_new.T, fc_bias - bias_vel_new, conv_vel_new, gamma_vel_new, beta_vel_new, fc_vel_new.T, bias_vel_new, loss_val)

    return jax.shard_map(local_step, mesh=mesh, in_specs=(P('dp'),) * 3 + (P(),) * 11, out_specs=(P(),) * 11, check_vma=False)
```

time: 2810 us -> 968 us (0.34)
  waiting for transfers between devices: 1860 us -> 53.8 us
  Pallas kernels: 0 us -> 403 us
  other arithmetic: 576 us -> 176 us
  matrix products: 297 us -> 229 us
    psum x2 -> x1, waiting for transfers between devices: 1860 us -> 53.7 us  [local_step(): g_conv, g_bias = lax.psum((d_conv, d_bias), 'dp')]
    pallas_call x0 -> x3, Pallas kernels: none -> 403 us  [the longest x1 296 us: fused_update(): pl.pallas_call(functools.partial(update_kernel, classes, rows_total), gri...]
    sub x2 -> x1, other arithmetic: 296 us -> 9.66 us  [local_step(): w_conv - conv_vel_new]
    reduce_sum x9, other arithmetic: 278 us -> 162 us  [the longest x1 57.6 us: local_step(): d_beta = jnp.sum(d_pre, axis=(0, 1))]
    dot_general x5 -> x4, matrix products: 297 us -> 229 us  [the longest x1 70.1 us: local_step(): jnp.dot(pooled_bf, fc_bf, preferred_element_type=jnp.float32) + fc_bias]
  transfers between devices with their start and end apart: 2 -> 3, of which waited for: 1 -> 1; matrix products, arithmetic and copies ran while one was open for 6% -> 32% of each run, Pallas kernels for 0% -> 0%
where the time goes in v1:
time: 968 us; the launch traced here: 962 us
  Pallas kernels  403 us (42%)
  matrix products  229 us (24%)
  other arithmetic  176 us (18%)
  waiting for transfers between devices  53.8 us (6%)
  blocking collectives  42 us (4%)
  local copies, waits for them, and re-layouts  38.2 us (4%)
  between operations  19.1 us (2%)
    pallas_call x1, Pallas kernels, fused_update(): pl.pallas_call(functools.partial(update_kernel, classes, rows_total), gri...  296 us
    pallas_call x1, Pallas kernels, shared_grads(): pl.pallas_call(functools.partial(grad_kernel, classes, rows_total), grid_...  92.9 us
    dot_general x1, matrix products, local_step(): jnp.dot(pooled_bf, fc_bf, preferred_element_type=jnp.float32) + fc_bias  70.1 us
    dot_general x1, matrix products, local_step(): jnp.einsum('bk,ck->bc', d_logits_bf, fc_bf, preferred_element_type=jnp.fl...  62.9 us
    reduce_sum x1, other arithmetic, local_step(): d_beta = jnp.sum(d_pre, axis=(0, 1))  57.6 us
    psum x1, waiting for transfers between devices, local_step(): g_conv, g_bias = lax.psum((d_conv, d_bias), 'dp')  53.7 us
    dot_general x1, matrix products, local_step(): jnp.einsum('bpc,bpd->cd', act_grid, d_conv_out.astype(jnp.bfloat16), pref...  52.8 us
    reduce_sum x1, other arithmetic, local_step(): pooled = jnp.mean(jax.nn.relu(pre_act), axis=1)  47 us
  transfers between devices with their start and end apart: 3, of which 1 were waited for; matrix products, arithmetic and copies ran while one was open for 32% of the time, Pallas kernels for 0%

profile of v1, /device:TPU:0, one launch (start us, length us, event | category | flops | bytes accessed | tf_op | source)
XLA Modules:
  0.0 961.7 jit_solution(11480291156670866298)
XLA Ops:
  7.2 0.0 all-gather.2.cloned.1.call-start
  7.2 43.4 %fusion.39 = (f32[2048]{0:T(1024)S(1)}, f32[256,49,2048]{2,0,1:T(8,128)}) fusion(bf16[256,49,512]{2,0,1:T(8,128)(2,1)} %bitcast.41, f32[512,2048]{1,0:T(8,128)} %param.17), kind=kOutput, calls=%fused_computation.63 | convolution fusion | flops 26333411328 | bytes 119808000 | tf_op jit(solution)/shard_map/bpc,cd->bpd/dot_general | solution.py:235
  50.7 0.0 copy-start.12
  50.7 31.1 %multiply_reduce_fusion = f32[2048]{0:T(1024)S(1)} fusion(f32[256,49,2048]{2,0,1:T(8,128)} %get-tuple-element.70, f32[2048]{0:T(1024)S(1)} %broadcast_multiply_fusion.4), kind=kLoop, calls=%fused_computation.9 | loop fusion | flops 77068288 | bytes 102776832 | tf_op jit(solution)/shard_map/reduce_sum | solution.py:238
  81.8 0.6 copy-done.14
  82.4 0.0 copy-done.4
  82.4 0.0 copy-done.8
  82.4 0.0 copy-done.12
  82.4 0.0 copy-start.10
  82.4 0.0 copy-start.18
  82.4 0.0 copy-start.1
  82.4 47.0 %maximum_reduce_fusion = f32[256,2048]{1,0:T(8,128)S(1)} fusion(bf16[256,7,7,2048]{3,0,2,1:T(8,128)(2,1)} %param.15, f32[2048]{0:T(1024)S(1)} %copy-done.12, f32[2048]{0:T(1024)S(1)} %copy-done.8, f32[2048]{0:T(1024)S(1)} %add_rsqrt_fusion, f32[256,49,2048]{2,0,1:T(8,128)} %get-tuple-element.70, f32[2048]{0:T(1024)S(1)} %broadcast_multiply_fusion.4), kind=kLoop, calls=%fused_computation.8 | loop fusion | flops 204996608 | bytes 156270592 | tf_op jit(solution)/shard_map/reduce_sum | solution.py:241
  129.4 0.0 copy-done.10
  129.4 1.5 broadcast_multiply_fusion
  130.9 0.0 all-gather.2.cloned.1.call-update
  130.9 0.2 all-reduce.5.cloned.1.call-start
  131.2 0.0 copy-done.18
  131.2 0.0 copy-done.1
  131.2 70.1 %fusion.40 = (f32[256]{0:T(256)S(1)}, f32[256,21843]{0,1:T(8,128)}) fusion(f32[21843]{0:T(1024)S(1)} %copy-done.1, f32[2048,21843]{0,1:T(8,128)} %param.20, f32[256,2048]{1,0:T(8,128)S(1)} %maximum_reduce_fusion), kind=kOutput, calls=%fused_computation.64 | convolution fusion | flops 22961010688 | bytes 203490640 | tf_op jit(solution)/shard_map/dot_general | solution.py:245
  201.3 10.4 %exponential_reduce_fusion = f32[256]{0:T(256)S(1)} fusion(f32[256,21843]{0,1:T(8,128)} %get-tuple-element.72, f32[256]{0:T(256)S(1)} %get-tuple-element.71), kind=kLoop, calls=%fused_computation.22 | loop fusion | flops 11183360 | bytes 22369280 | tf_op jit(solution)/shard_map/reduce_sum | solution.py:247
  211.7 3.5 copy-done
  215.2 6.4 multiply_reduce_fusion.1
  223.0 13.6 %all_gather.7 = f32[2048,2]{0,1:T(2,128)S(1)} all-gather(f32[256,2]{0,1:T(2,128)S(1)} %pad_maximum_fusion), channel_id=1, replica_groups=mesh['dp'=8] {'dp'}, dimensions={0}, use_global_device_ids=true | all-gather | bytes 18432 | tf_op jit(solution)/shard_map/all_gather | solution.py:260
  236.5 0.6 pad_add_fusion.sc
  237.1 0.6 fusion.28
  237.7 14.3 %round_both.1 = (bf16[2048,2048]{1,0:T(8,128)(2,1)}, bf16[2048,2048]{1,0:T(8,128)(2,1)}) custom-call(f32[2048,2048]{1,0:T(8,128)} %all-gather.2.cloned.1.call-done.x), custom_call_target="tpu_custom_call" | custom-call | flops 8388608 | bytes 33554432 | tf_op jit(solution)/shard_map/round_both/pallas_call | solution.py:208
  252.0 10.3 %broadcast_in_dim.13.refs_9_.refs_10_.refs_11_.bias = f32[22016,128]{1,0:T(8,128)} broadcast(f32[22016]{0:T(1024)S(1)} %pad.4), dimensions={0} | broadcast | bytes 11360256 | tf_op jit(solution)/shard_map/broadcast_in_dim | solution.py:266
  262.3 0.0 copy-done.16
  262.3 92.9 %shared_grads.1 = (f32[45,96,2048]{2,1,0:T(8,128)}, f32[45,96,128]{2,1,0:T(8,128)}, f32[2,8,2048]{2,1,0:T(8,128)}) custom-call(s32[2]{0:T(128)} %pad_add_fusion.sc, f32[21843,2048]{1,0:T(8,128)} %bitcast.7.refs_0_.refs_1_.refs_2_.refs_3_.refs_4_.refs_5_.refs_6_.refs_7_.refs_8_.w_in, ...), custom_call_target="tpu_custom_call" | custom-call | flops 72477573120 | bytes 70778880 | tf_op jit(solution)/shard_map/shared_grads/pallas_call | solution.py:105
  355.2 0.0 copy-start.5
  355.2 0.0 copy-start.9
  355.2 0.0 copy-start.11
  355.3 0.0 copy-start.13
  355.3 0.0 collective-permute-start
  355.3 0.0 copy-done.17
  355.3 0.0 copy-done.19
  355.3 62.9 %fusion.21 = f32[256,2048]{1,0:T(8,128)S(1)} fusion(f32[2048,21843]{0,1:T(8,128)} %param.20, f32[256,21843]{0,1:T(8,128)} %get-tuple-element.72, s32[256]{0:T(256)S(1)} %copy-done.19, f32[256]{0:T(256)S(1)} %copy-done.17), kind=kOutput, calls=%fused_computation.32 | convolution fusion | flops 22982854656 | bytes 203404288 | tf_op jit(solution)/shard_map/bk,ck->bc/dot_general | solution.py:253
  418.3 0.0 copy-done.5
  418.3 0.0 copy-start.3
  418.3 0.0 copy-start.15
  418.3 0.0 copy-start.20
  418.3 57.6 %select_reduce_fusion = (f32[2048]{0:T(1024)S(1)}, f32[2048]{0:T(1024)S(1)}, pred[256,49,2048]{2,0,1:T(32,128)(4,1)}) fusion(f32[256,2048]{1,0:T(8,128)S(1)} %fusion.21, f32[2048]{0:T(1024)S(1)} %copy-done.11, f32[256,49,2048]{2,0,1:T(8,128)} %get-tuple-element.70, f32[2048]{0:T(1024)S(1)} %copy-done.5, bf16[256,7,7,2048]{3,0,2,1:T(8,128)(2,1)} %param.15, ...), kind=kLoop, calls=%fused_computation.2 | loop fusion | flops 282587136 | bytes 181977088 | tf_op jit(solution)/shard_map/reduce_sum | solution.py:255
  475.9 0.1 reduce_sum.107
  476.0 1.8 slice_reduce_fusion
  477.9 1.1 dynamic_update_slice.3
  479.0 0.7 reshape.95
  479.7 28.4 %all-reduce.1 = (f32[2048]{0:T(1024)S(1)}, f32[2048]{0:T(1024)S(1)}, f32[2]{0:T(128)S(1)}, f32[]{:T(128)}) all-reduce(f32[2048]{0:T(1024)S(1)} %get-tuple-element.48, f32[2048]{0:T(1024)S(1)} %get-tuple-element.47, f32[2]{0:T(128)S(1)} %reduce_sum.107, f32[]{:T(128)S(6)} %div.65), channel_id=1, replica_groups=mesh['dp'=8] {'dp'}, use_global_device_ids=true, to_apply=%region_10.11 | all-reduce | flops 4099 | bytes 32792 | tf_op jit(solution)/shard_map/psum | solution.py:274
  508.1 0.6 fusion.36
  508.7 52.8 %fusion.18 = f32[512,2048]{0,1:T(8,128)} fusion(bf16[256,49,512]{2,0,1:T(8,128)(2,1)} %bitcast.42, pred[256,49,2048]{2,0,1:T(32,128)(4,1)} %get-tuple-element.63, f32[256,49,2048]{2,0,1:T(8,128)} %get-tuple-element.70, f32[2048]{0:T(1024)S(1)} %get-tuple-element.73, f32[2048]{0:T(1024)S(1)} %get-tuple-element.74, f32[256,2048]{1,0:T(8,128)S(1)} %fusion.21, ...), kind=kOutput, calls=%fused_computation.31 | convolution fusion | flops 26512195584 | bytes 147628032 | tf_op jit(solution)/shard_map/bpc,bpd->cd/dot_general | solution.py:258
  561.5 0.0 all-reduce.5.cloned.1.call-update
  561.5 5.3 copy.34
  566.9 3.9 multiply_reduce_fusion.3
  571.4 5.3 copy.31
  576.8 0.6 fusion.38
  578.8 0.6 fusion.35
  579.4 53.7 %all-reduce.5.cloned.1.call-done = (f32[512,2048]{0,1:T(8,128)}, f32[21843]{0:T(1024)}) async-done(((f32[512,2048]{0,1:T(8,128)}, f32[21843]{0:T(1024)}), (f32[512,2048]{0,1:T(8,128)}, f32[21843]{0:T(1024)})) %all-reduce.5.cloned.1.call-update) | async-done | bytes 4281692 | tf_op jit(solution)/shard_map/psum | solution.py:275
  633.1 3.9 multiply_reduce_fusion.2
  637.8 9.7 %fusion.37 = (f32[512,2048]{0,1:T(8,128)}, f32[512,2048]{0,1:T(8,128)}) fusion(f32[512,2048]{0,1:T(8,128)} %copy.34, f32[512,2048]{0,1:T(8,128)} %get-tuple-element.53, f32[]{:T(128)S(6)} %mul.131, f32[512,2048]{0,1:T(8,128)} %copy.31), kind=kLoop, calls=%fused_computation.61 | loop fusion | flops 6291456 | bytes 20971524 | tf_op jit(solution)/shard_map/sub | solution.py:286
  647.4 5.3 copy.35
  652.8 5.3 copy.36
  658.1 0.0 copy-done.7
  658.1 0.7 fusion.34
  658.8 0.0 collective-permute-done.other
  658.8 295.5 %fused_update.1 = (f32[21843,2048]{1,0:T(8,128)}, f32[21843,2048]{1,0:T(8,128)}) custom-call(s32[2]{0:T(128)} %pad_add_fusion.sc, f32[1]{0:T(128)} %bitcast.14.rate, f32[21843,2048]{1,0:T(8,128)} %bitcast.7.refs_0_.refs_1_.refs_2_.refs_3_.refs_4_.refs_5_.refs_6_.refs_7_.refs_8_.w_in, f32[21843,2048]{1,0:T(8,128)} %bitcast.15.v_in, ...), custom_call_target="tpu_custom_call" | custom-call | flops 230854492160 | bytes 715751424 | tf_op jit(solution)/shard_map/fused_update/pallas_call | solution.py:182
  (31 shorter events, 0.1 us)
Async XLA Ops:
  7.2 230.5 %all-gather.2.cloned.1.call-start = ((), (), s32[]{:S(2)}) async-start(), calls=%async_computation | async-start | bytes 18874368 | tf_op jit(solution)/shard_map/all_gather | solution.py:243
  50.7 31.7 %copy-start.4 = (f32[2048]{0:T(1024)}, f32[2048]{0:T(1024)S(1)}, u32[]{:S(2)}) copy-start(f32[2048]{0:T(1024)S(1)} %broadcast_multiply_fusion.4) | copy-start | bytes 24580
  50.7 31.7 %copy-start.8 = (f32[2048]{0:T(1024)S(1)}, f32[2048]{0:T(1024)}, u32[]{:S(2)}) copy-start(f32[2048]{0:T(1024)} %param.18) | copy-start | bytes 24580
  50.7 31.7 %copy-start.12 = (f32[2048]{0:T(1024)S(1)}, f32[2048]{0:T(1024)}, u32[]{:S(2)}) copy-start(f32[2048]{0:T(1024)} %param.19) | copy-start | bytes 24580
  81.8 0.6 copy-start.14
  82.4 47.0 %copy-start.10 = (f32[2048]{0:T(1024)}, f32[2048]{0:T(1024)S(1)}, u32[]{:S(2)}) copy-start(f32[2048]{0:T(1024)S(1)} %add_rsqrt_fusion) | copy-start | bytes 24580
  82.4 48.8 %copy-start.18 = (s32[256]{0:T(256)S(1)}, s32[256]{0:T(256)}, u32[]{:S(2)}) copy-start(s32[256]{0:T(256)} %param.16) | copy-start | bytes 3076
  82.4 48.8 %copy-start.1 = (f32[21843]{0:T(1024)S(1)}, f32[21843]{0:T(1024)}, u32[]{:S(2)}) copy-start(f32[21843]{0:T(1024)} %param.21) | copy-start | bytes 262120
  130.9 502.2 %all-reduce.5.cloned.1.call-start = ((), (), s32[]{:S(2)}) async-start(), calls=%async_computation.1 | async-start | bytes 8568832 | tf_op jit(solution)/shard_map/psum | solution.py:275
  201.3 13.9 %copy-start = (f32[256,21843]{0,1:T(8,128)S(1)}, f32[256,21843]{0,1:T(8,128)}, u32[]{:S(2)}) copy-start(f32[256,21843]{0,1:T(8,128)} %get-tuple-element.72) | copy-start | bytes 67101700
  215.2 47.1 %copy-start.16 = (f32[256]{0:T(256)}, f32[256]{0:T(256)S(1)}, u32[]{:S(2)}) copy-start(f32[256]{0:T(256)S(1)} %log_add_fusion) | copy-start | bytes 3076
  262.3 93.0 %copy-start.17 = (f32[256]{0:T(256)S(1)}, f32[256]{0:T(256)}, u32[]{:S(2)}) copy-start(f32[256]{0:T(256)} %copy-done.16) | copy-start | bytes 3076
  262.3 93.0 %copy-start.19 = (s32[256]{0:T(256)S(1)}, s32[256]{0:T(256)}, u32[]{:S(2)}) copy-start(s32[256]{0:T(256)} %param.16) | copy-start | bytes 3076
  355.2 63.1 %copy-start.5 = (f32[2048]{0:T(1024)S(1)}, f32[2048]{0:T(1024)}, u32[]{:S(2)}) copy-start(f32[2048]{0:T(1024)} %copy-done.4) | copy-start | bytes 24580
  355.2 63.0 %copy-start.9 = (f32[2048]{0:T(1024)S(1)}, f32[2048]{0:T(1024)}, u32[]{:S(2)}) copy-start(f32[2048]{0:T(1024)} %param.18) | copy-start | bytes 24580
  355.2 63.0 %copy-start.11 = (f32[2048]{0:T(1024)S(1)}, f32[2048]{0:T(1024)}, u32[]{:S(2)}) copy-start(f32[2048]{0:T(1024)} %copy-done.10) | copy-start | bytes 24580
  355.3 63.0 %copy-start.13 = (f32[2048]{0:T(1024)S(1)}, f32[2048]{0:T(1024)}, u32[]{:S(2)}) copy-start(f32[2048]{0:T(1024)} %param.19) | copy-start | bytes 24580
  355.3 303.6 %collective-permute-start = (f32[45,96,2048]{2,1,0:T(8,128)}, f32[45,96,2048]{2,1,0:T(8,128)}, u32[]{:S(2)}, u32[]{:S(2)}) collective-permute-start(f32[45,96,2048]{2,1,0:T(8,128)} %get-tuple-element.21.own), channel_id=1, source_target_pairs={{0,1},{1,0},{2,3},{3,2},{4,5},{5,4},{6,7},{7,6}} | collective-permute-start | bytes 106168328 | tf_op jit(solution)/shard_map/ppermute | solution.py:268
  418.3 57.6 %copy-start.3 = (f32[2,8,2048]{2,1,0:T(8,128)S(1)}, f32[2,8,2048]{2,1,0:T(8,128)}, u32[]{:S(2)}) copy-start(f32[2,8,2048]{2,1,0:T(8,128)} %get-tuple-element.20) | copy-start | bytes 393220
  418.3 89.8 %copy-start.15 = (f32[2048]{0:T(1024)S(1)}, f32[2048]{0:T(1024)}, u32[]{:S(2)}) copy-start(f32[2048]{0:T(1024)} %copy-done.14) | copy-start | bytes 24580
  418.3 89.8 %copy-start.20 = (f32[2048]{0:T(1024)S(1)}, f32[2048]{0:T(1024)}, u32[]{:S(2)}) copy-start(f32[2048]{0:T(1024)} %param.23) | copy-start | bytes 24580
  561.5 17.3 %copy-start.21 = (f32[2048]{0:T(1024)S(1)}, f32[2048]{0:T(1024)}, u32[]{:S(2)}) copy-start(f32[2048]{0:T(1024)} %param.24) | copy-start | bytes 24580
  576.8 81.4 %copy-start.2 = (f32[21843]{0:T(1024)S(1)}, f32[21843]{0:T(1024)}, u32[]{:S(2)}) copy-start(f32[21843]{0:T(1024)} %param.21) | copy-start | bytes 262120
  576.8 81.4 %copy-start.6 = (f32[21843]{0:T(1024)S(1)}, f32[21843]{0:T(1024)}, u32[]{:S(2)}) copy-start(f32[21843]{0:T(1024)} %param.26) | copy-start | bytes 262120
  633.1 25.0 %copy-start.7 = (f32[21843]{0:T(1024)S(1)}, f32[21843]{0:T(1024)}, u32[]{:S(2)}) copy-start(f32[21843]{0:T(1024)} %get-tuple-element.54) | copy-start | bytes 262120
Sparse Core Ops, SparseCore 0:
  131.1 86.8 all-gather.1
  561.6 71.4 all-reduce.4

commit v2 on v0

v2 whole, which is shorter than its diff:
```python
import functools

import jax
import jax.numpy as jnp
from jax import lax
from jax.experimental import pallas as pl
from jax.experimental.pallas import tpu as pltpu
from jax.sharding import PartitionSpec as P

BN_EPS = 1e-5
SMOOTHING = 0.1
MOMENTUM = 0.9
TRUST_COEF = 0.001
WEIGHT_DECAY = 5e-5

TILE = 256
BLK = 32
SLOTS = TILE // BLK
HAVE = 3
NORM = 2
GROUP = 3
CHUNK = 512
POS = 7
WIDTH = 512
LANES = 128
SUB = 8
RING = 4
VMEM_LIMIT = 66_000_000


def aligned(i, size):
    return pl.ds(pl.multiple_of(i, size), size)


def tiled(x, reps):
    return jnp.concatenate([x] * reps, axis=1)


def logit_grads(z, bias, lse, lab, base, classes):
    cols = z.shape[1]
    row = (lax.broadcasted_iota(jnp.int32, (BLK, cols), 0) + base).astype(jnp.float32)
    e = jnp.exp(z + tiled(bias, cols // LANES) - lse)
    low = SMOOTHING / classes
    return e - jnp.where(lab == row, low + (1.0 - SMOOTHING), low)


def grad_kernel(classes, groups, steps, *refs):
    nw = GROUP * HAVE
    ws, biases = refs[:nw], refs[nw:nw + GROUP]
    (p_all, own, lr, g_out, p_out, db_out, rows_out, rate_out, p, pbuf, lhs, dmat, gbuf, meta, sq, msg, msgs,
     p_sem, keep_sem, g_sem, gs_sem, gr_sem, meta_s, meta_r, msg_s, msg_r) = refs[nw + GROUP:]
    me = lax.axis_index('dp')
    q, c = me // 2, me % 2
    step = pl.program_id(0)
    rows_total, feats = p.shape
    per_dev = rows_total // groups

    def slot_of(i):
        return (2 * q + i) % SLOTS

    def base_of(group, k):
        return (2 * (GROUP * group + k // HAVE) + c) * TILE + slot_of(k % HAVE) * BLK

    def prepare(group):
        for k in range(nw):
            valid = lax.broadcasted_iota(jnp.int32, (BLK, feats), 0) < classes - base_of(group, k)
            w = jnp.where(valid, ws[k][...], 0.0)
            if k % HAVE < NORM:
                sq[1] += jnp.sum((w * w).reshape(BLK // 8, 8, feats), axis=0)
            lhs[group % 2, k * BLK:(k + 1) * BLK, :] = w.astype(jnp.bfloat16)

    def local(group):
        return pltpu.make_async_copy(gbuf.at[group % 2], g_out.at[c, pl.ds(group * GROUP, GROUP)], g_sem.at[group % 2])

    def remote(group):
        return pltpu.make_async_remote_copy(
            gbuf.at[group % 2], g_out.at[c, pl.ds(group * GROUP, GROUP)], gs_sem.at[group % 2], gr_sem.at[group],
            device_id=(me + 1 - 2 * c,), device_id_type=pl.DeviceIdType.MESH)

    def arrival(group):
        return pltpu.make_async_remote_copy(
            gbuf.at[group % 2], g_out.at[1 - c, pl.ds(group * GROUP, GROUP)], gs_sem.at[group % 2], gr_sem.at[group],
            device_id=(me + 1 - 2 * c,), device_id_type=pl.DeviceIdType.MESH)

    def spread(src, dst, send, recv):
        return [pltpu.make_async_remote_copy(
            src, dst.at[me], send.at[o], recv.at[o],
            device_id=((me + o) % groups,), device_id_type=pl.DeviceIdType.MESH) for o in range(1, groups)]

    keep = pltpu.make_async_copy(p, p_out, keep_sem)

    @pl.when(step == 0)
    def _():
        def fetch(i, slot):
            return pltpu.make_async_copy(p_all.at[aligned(i * per_dev, per_dev)], pbuf.at[slot], p_sem.at[slot])

        fetch(0, 0).start()
        barrier = pltpu.get_barrier_semaphore()
        for o in range(1, groups):
            pl.semaphore_signal(barrier, 1, device_id=((me + o) % groups,), device_id_type=pl.DeviceIdType.MESH)
        pl.semaphore_wait(barrier, groups - 1)
        for copy in spread(own, meta, meta_s, meta_r):
            copy.start()
        meta[me] = own[...]
        sq[...] = jnp.zeros_like(sq)
        prepare(0)

        def convert(i, carry):
            @pl.when(i + 1 < groups)
            def _():
                fetch(i + 1, (i + 1) % 2).start()
            fetch(i, i % 2).wait()
            at = aligned(i * per_dev, per_dev)
            p[at, :] = pbuf[i % 2].astype(jnp.bfloat16)
            return carry

        lax.fori_loop(0, groups, convert, 0)
        keep.start()
        for copy in spread(own, meta, meta_s, meta_r):
            copy.wait()
        for d in range(groups):
            rows_out[:, d * per_dev:(d + 1) * per_dev] = meta[d]

    @pl.when(step > 1)
    def _():
        local(step - 2).start()
        remote(step - 2).start()

    @pl.when(step > 2)
    def _():
        local(step - 3).wait()
        remote(step - 3).wait_send()

    @pl.when(step > 0)
    def _():
        group = step - 1
        now = group % 2
        prepare(step)
        sums = [jnp.zeros((BLK, LANES), jnp.float32) for _ in range(nw)]
        for n in range(rows_total // CHUNK):
            cs = slice(n * CHUNK, (n + 1) * CHUNK)
            z = lax.dot_general(lhs[now], p[cs, :], (((1,), (1,)), ((), ())), preferred_element_type=jnp.float32)
            for k in range(nw):
                rs = slice(k * BLK, (k + 1) * BLK)
                bias = biases[k // HAVE][aligned(slot_of(k % HAVE) * BLK, BLK), :]
                d = logit_grads(z[rs], bias, rows_out[0:1, cs], rows_out[1:2, cs], base_of(group, k), classes)
                valid = lax.broadcasted_iota(jnp.int32, (BLK, CHUNK), 0) < classes - base_of(group, k)
                d = jnp.where(valid, d, 0.0)
                for m in range(CHUNK // LANES):
                    sums[k] = sums[k] + d[:, m * LANES:(m + 1) * LANES]
                dmat[rs, cs] = d.astype(jnp.bfloat16)
        for k in range(nw):
            db_out[k // HAVE, (k % HAVE) * BLK:(k % HAVE + 1) * BLK, :] = sums[k]
        for n in range(feats // CHUNK):
            cs = slice(n * CHUNK, (n + 1) * CHUNK)
            g = jnp.dot(dmat[...], p[:, cs], preferred_element_type=jnp.float32) * (1.0 / rows_total)
            for k in range(nw):
                gk = g[k * BLK:(k + 1) * BLK]
                gbuf[now, k // HAVE, (k % HAVE) * BLK:(k % HAVE + 1) * BLK, cs] = gk
                if k % HAVE < NORM:
                    sq[0, :, cs] += jnp.sum((gk * gk).reshape(BLK // 8, 8, CHUNK), axis=0)

    @pl.when(step == steps)
    def _():
        for i in range(2):
            parts = sq[i]
            total = parts[:, 0:LANES]
            for m in range(1, feats // LANES):
                total = total + parts[:, m * LANES:(m + 1) * LANES]
            msg[i] = total
        local(steps - 1).start()
        remote(steps - 1).start()
        for group in (steps - 2, steps - 1):
            local(group).wait()
            remote(group).wait_send()
        keep.wait()
        for copy in spread(msg, msgs, msg_s, msg_r):
            copy.start()
        msgs[me] = msg[...]
        for group in range(steps):
            arrival(group).wait_recv()
        for copy in spread(msg, msgs, msg_s, msg_r):
            copy.wait()
        both = jnp.sum(msgs[...], axis=0)
        g_norm = jnp.sqrt(jnp.sum(both[0]))
        w_norm = jnp.sqrt(jnp.sum(both[1]))
        rate_out[...] = jnp.full(rate_out.shape, lr[0] * TRUST_COEF * w_norm / (g_norm + WEIGHT_DECAY * w_norm), jnp.float32)


def shared_grads(groups, wt, bias, p_all, own, lr):
    classes, feats = wt.shape
    rows_total = p_all.shape[0]
    n_tiles = pl.cdiv(classes, TILE)
    steps = pl.cdiv(pl.cdiv(n_tiles, 2), GROUP)
    last = pl.cdiv(classes, BLK) - 1

    def w_map(t, i):
        def index(s):
            me = lax.axis_index('dp')
            tile = 2 * (GROUP * jnp.minimum(s, steps - 1) + t) + me % 2
            return jnp.minimum(tile * SLOTS + (2 * (me // 2) + i) % SLOTS, last), 0
        return index

    def b_map(t):
        return lambda s: (jnp.minimum(2 * (GROUP * jnp.maximum(s - 1, 0) + t) + lax.axis_index('dp') % 2, n_tiles - 1), 0)

    rows = GROUP * HAVE * BLK
    anywhere = pl.BlockSpec(memory_space=pl.ANY)
    dma = pltpu.SemaphoreType.DMA
    return pl.pallas_call(
        functools.partial(grad_kernel, classes, groups, steps),
        grid=(steps + 1,),
        in_specs=[pl.BlockSpec((BLK, feats), w_map(t, i)) for t in range(GROUP) for i in range(HAVE)]
        + [pl.BlockSpec((TILE, LANES), b_map(t)) for t in range(GROUP)]
        + [anywhere, pl.BlockSpec(own.shape, lambda s: (0, 0)), pl.BlockSpec(memory_space=pltpu.SMEM)],
        out_specs=[
            anywhere, anywhere,
            pl.BlockSpec((GROUP, HAVE * BLK, LANES), lambda s: (jnp.maximum(s - 1, 0), 0, 0)),
            pl.BlockSpec((8, rows_total), lambda s: (0, 0)),
            pl.BlockSpec((8, LANES), lambda s: (0, 0)),
        ],
        out_shape=[
            jax.ShapeDtypeStruct((2, steps * GROUP, HAVE * BLK, feats), jnp.float32),
            jax.ShapeDtypeStruct((rows_total, feats), jnp.bfloat16),
            jax.ShapeDtypeStruct((steps * GROUP, HAVE * BLK, LANES), jnp.float32),
            jax.ShapeDtypeStruct((8, rows_total), jnp.float32),
            jax.ShapeDtypeStruct((8, LANES), jnp.float32),
        ],
        scratch_shapes=[
            pltpu.VMEM((rows_total, feats), jnp.bfloat16),
            pltpu.VMEM((2, rows_total // groups, feats), jnp.float32),
            pltpu.VMEM((2, rows, feats), jnp.bfloat16), pltpu.VMEM((rows, rows_total), jnp.bfloat16),
            pltpu.VMEM((2, GROUP, HAVE * BLK, feats), jnp.float32),
            pltpu.VMEM((groups,) + own.shape, jnp.float32),
            pltpu.VMEM((2, 8, feats), jnp.float32), pltpu.VMEM((2, 8, LANES), jnp.float32), pltpu.VMEM((groups, 2, 8, LANES), jnp.float32),
            dma((2,)), dma, dma((2,)), dma((2,)), dma((steps,)),
            dma((groups,)), dma((groups,)), dma((groups,)), dma((groups,)),
        ],
        compiler_params=pltpu.CompilerParams(dimension_semantics=("arbitrary",), vmem_limit_bytes=VMEM_LIMIT, collective_id=0, has_side_effects=True),
        cost_estimate=pl.CostEstimate(flops=4 * steps * rows * feats * rows_total, bytes_accessed=8 * steps * rows * feats, transcendentals=0),
        name="shared_grads",
    )(*([wt] * (GROUP * HAVE)), *([bias] * GROUP), p_all, own, lr)


def update_kernel(classes, rows_total, rate, w_in, v_in, even, odd, bias, p, rows_in, w_out, v_out, done, lhs, dmat):
    q = lax.axis_index('dp') // 2
    step = pl.program_id(0)
    a = tiled(rate[0:1, :], CHUNK // LANES)
    cols, feats = p.shape
    done[...] = jnp.zeros_like(done)

    def rows_at(base):
        return aligned(base, BLK)

    def apply(rs, cs, g):
        w = w_in[rs, cs]
        nv = MOMENTUM * v_in[rs, cs] + a * (g + WEIGHT_DECAY * w)
        v_out[rs, cs] = nv
        w_out[rs, cs] = w - nv

    bases = []
    for t in range(2):
        for i in range(HAVE, SLOTS):
            bases.append(t * TILE + (2 * q + i) % SLOTS * BLK)
    for k, base in enumerate(bases):
        lhs[k * BLK:(k + 1) * BLK, :] = w_in[rows_at(base), :].astype(jnp.bfloat16)
    for n in range(cols // CHUNK):
        cs = slice(n * CHUNK, (n + 1) * CHUNK)
        z = lax.dot_general(lhs[...], p[cs, :], (((1,), (1,)), ((), ())), preferred_element_type=jnp.float32)
        for t, src in enumerate((even, odd)):
            for i in range(HAVE):
                apply(rows_at(t * TILE + (2 * q + i) % SLOTS * BLK), cs, src[0, 0, i * BLK:(i + 1) * BLK, cs])
        for k, base in enumerate(bases):
            rs = slice(k * BLK, (k + 1) * BLK)
            d = logit_grads(z[rs], bias[rows_at(base), :], rows_in[0:1, cs], rows_in[1:2, cs], step * 2 * TILE + base, classes)
            dmat[rs, cs] = d.astype(jnp.bfloat16)
    for n in range(feats // CHUNK):
        cs = slice(n * CHUNK, (n + 1) * CHUNK)
        g = jnp.dot(dmat[...], p[:, cs], preferred_element_type=jnp.float32) * (1.0 / rows_total)
        for k, base in enumerate(bases):
            apply(rows_at(base), cs, g[k * BLK:(k + 1) * BLK])


def fused_update(rate, wt, vt, grads, bias, p, rows_in):
    classes, feats = wt.shape
    rows_total = p.shape[0]
    steps = pl.cdiv(classes, 2 * TILE)
    once = dict(pipeline_mode=pl.Buffered(1))
    whole = lambda a: pl.BlockSpec(a.shape, lambda s: (0, 0), **once)
    tile = pl.BlockSpec((2 * TILE, feats), lambda s: (s, 0))
    part = lambda par: pl.BlockSpec((1, 1, HAVE * BLK, feats), lambda s: (par, s, 0, 0))
    rows = 2 * (SLOTS - HAVE) * BLK
    return pl.pallas_call(
        functools.partial(update_kernel, classes, rows_total),
        grid=(steps,),
        in_specs=[whole(rate), tile, tile, part(0), part(1), pl.BlockSpec((2 * TILE, LANES), lambda s: (s, 0)), whole(p), whole(rows_in)],
        out_specs=[tile, tile, pl.BlockSpec((8, LANES), lambda s: (0, 0))],
        scratch_shapes=[pltpu.VMEM((rows, feats), jnp.bfloat16), pltpu.VMEM((rows, rows_total), jnp.bfloat16)],
        out_shape=[jax.ShapeDtypeStruct(wt.shape, jnp.float32)] * 2 + [jax.ShapeDtypeStruct((8, LANES), jnp.float32)],
        compiler_params=pltpu.CompilerParams(dimension_semantics=("arbitrary",), vmem_limit_bytes=VMEM_LIMIT),
        cost_estimate=pl.CostEstimate(flops=4 * steps * rows * feats * rows_total, bytes_accessed=16 * classes * feats, transcendentals=0),
        name="fused_update",
    )(rate, wt, vt, grads, grads, bias, p, rows_in)


def conv_update_kernel(dep, lr, g_hbm, w_hbm, v_hbm, w_out, v_out, g, w, v, sem, out_sem):
    loads = [pltpu.make_async_copy(x, y, sem.at[i]) for i, (x, y) in enumerate(((g_hbm, g), (w_hbm, w), (v_hbm, v)))]
    for copy in loads:
        copy.start()
    parts = out_sem.shape[1]
    size = g.shape[0] // parts

    def square_sum(ref):
        def add(i, acc):
            x = ref[aligned(i * size, size)]
            return acc + jnp.sum((x * x).reshape(size // SUB, SUB, x.shape[1]), axis=0)
        return jnp.sum(lax.fori_loop(0, parts, add, jnp.zeros((SUB, ref.shape[1]), jnp.float32)))

    loads[0].wait()
    g_norm = jnp.sqrt(square_sum(g))
    loads[1].wait()
    w_norm = jnp.sqrt(square_sum(w))
    loads[2].wait()
    rate = lr[0] * TRUST_COEF * w_norm / (g_norm + WEIGHT_DECAY * w_norm)

    def stores(i):
        at = aligned(i * size, size)
        return [pltpu.make_async_copy(w.at[at], w_out.at[at], out_sem.at[0, i]), pltpu.make_async_copy(v.at[at], v_out.at[at], out_sem.at[1, i])]

    def update(i, carry):
        at = aligned(i * size, size)
        nv = MOMENTUM * v[at] + rate * (g[at] + WEIGHT_DECAY * w[at])
        v[at] = nv
        w[at] = w[at] - nv
        for copy in stores(i):
            copy.start()
        return carry

    def finish(i, carry):
        for copy in stores(i):
            copy.wait()
        return carry

    lax.fori_loop(0, parts, update, 0)
    lax.fori_loop(0, parts, finish, 0)


def conv_update(dep, lr, g, w, v):
    anywhere = pl.BlockSpec(memory_space=pl.ANY)
    dma = pltpu.SemaphoreType.DMA
    return pl.pallas_call(
        conv_update_kernel,
        in_specs=[pl.BlockSpec(memory_space=pltpu.VMEM), pl.BlockSpec(memory_space=pltpu.SMEM), anywhere, anywhere, anywhere],
        out_specs=[anywhere, anywhere],
        out_shape=[jax.ShapeDtypeStruct(w.shape, jnp.float32)] * 2,
        scratch_shapes=[pltpu.VMEM(w.shape, jnp.float32)] * 3 + [dma((3,)), dma((2, 8))],
        compiler_params=pltpu.CompilerParams(vmem_limit_bytes=VMEM_LIMIT),
        cost_estimate=pl.CostEstimate(flops=10 * w.size, bytes_accessed=20 * w.size, transcendentals=0),
        name="conv_update",
    )(dep, lr, g, w, v)


def gram_kernel(pos_count, scans, a, wc, gamma, beta, gcw_out, stats_out, asum_out, wb_out, gram, asum, parts):
    step = pl.program_id(0)
    c_mid = a.shape[-1]
    cols = wc.shape[1]

    @pl.when(step == 0)
    def _():
        gram[...] = jnp.zeros_like(gram)
        asum[...] = jnp.zeros_like(asum)

    @pl.when(step < scans)
    def _():
        x = a[...].reshape(-1, c_mid)
        gram[...] += lax.dot_general(x, x, (((0,), (0,)), ((), ())), preferred_element_type=jnp.float32)
        asum[...] += jnp.sum(x.astype(jnp.float32).reshape(-1, SUB, c_mid), axis=0)

    @pl.when(step == scans)
    def _():
        total = jnp.sum(asum[...], axis=0, keepdims=True)
        col = jnp.broadcast_to(total, (LANES, c_mid)).T
        asum_out[...] = col
        rest = gram[...] - tiled(col, c_mid // LANES) * (total / pos_count)
        for i in range(parts.shape[0]):
            part = rest.astype(jnp.bfloat16)
            parts[i] = part
            rest = rest - part.astype(jnp.float32)

    @pl.when(step >= scans)
    def _():
        wb = wc[...].astype(jnp.bfloat16)
        wb_out[...] = wb
        wr = wb.astype(jnp.float32)
        gcw = jnp.zeros((c_mid, cols), jnp.float32)
        for i in reversed(range(parts.shape[0])):
            gcw = gcw + jnp.dot(parts[i], wb, preferred_element_type=jnp.float32)
        gcw_out[...] = gcw
        var = jnp.maximum(jnp.sum(wr * gcw, axis=0, keepdims=True) / pos_count, 0.0)
        mean = jnp.sum(wr * tiled(asum_out[...], cols // LANES), axis=0, keepdims=True) / pos_count
        inv = lax.rsqrt(var + BN_EPS)
        scale = gamma[...] * inv
        stats_out[...] = stack_rows(mean, inv, scale, beta[...] - mean * scale)


def stack_rows(*rows):
    return jnp.concatenate(rows + (jnp.zeros_like(rows[0]),) * (SUB - len(rows)), axis=0)


def batch_stats(a3, w_conv, gamma, beta):
    spatial, per_dev, c_mid = a3.shape
    c_out = w_conv.shape[1]
    pos_count = spatial * per_dev
    scans = spatial // POS
    chunk = lambda rows: pl.BlockSpec((rows, CHUNK), lambda i: (0, jnp.maximum(i - scans, 0)))
    return pl.pallas_call(
        functools.partial(gram_kernel, pos_count, scans),
        grid=(scans + c_out // CHUNK,),
        in_specs=[pl.BlockSpec((POS, per_dev, c_mid), lambda i: (jnp.minimum(i, scans - 1), 0, 0)), chunk(c_mid), chunk(1), chunk(1)],
        out_specs=[chunk(c_mid), chunk(SUB), pl.BlockSpec((c_mid, LANES), lambda i: (0, 0)), chunk(c_mid)],
        out_shape=[
            jax.ShapeDtypeStruct((c_mid, c_out), jnp.float32),
            jax.ShapeDtypeStruct((SUB, c_out), jnp.float32),
            jax.ShapeDtypeStruct((c_mid, LANES), jnp.float32),
            jax.ShapeDtypeStruct((c_mid, c_out), jnp.bfloat16),
        ],
        scratch_shapes=[pltpu.VMEM((c_mid, c_mid), jnp.float32), pltpu.VMEM((SUB, c_mid), jnp.float32), pltpu.VMEM((3, c_mid, c_mid), jnp.bfloat16)],
        compiler_params=pltpu.CompilerParams(dimension_semantics=("arbitrary",), vmem_limit_bytes=VMEM_LIMIT),
        cost_estimate=pl.CostEstimate(flops=2 * pos_count * c_mid * c_mid, bytes_accessed=2 * pos_count * c_mid, transcendentals=0),
        name="batch_stats",
    )(a3, w_conv, gamma[None, :], beta[None, :])


def pool_kernel(spatial, a, s, wb, stats, p_out, n_out, mask_out):
    step = pl.program_id(0)
    wide = 2 * CHUNK

    @pl.when(step == 0)
    def _():
        p_out[...] = jnp.zeros_like(p_out)
        n_out[...] = jnp.zeros_like(n_out)

    def chunk(n, carry):
        cs = aligned(n * wide, wide)
        scale, shift = stats[2:3, cs], stats[3:4, cs]
        for j in range(POS):
            z = jnp.dot(a[j], wb[:, cs], preferred_element_type=jnp.float32)
            y = jnp.maximum(z * scale + shift + s[j, :, cs].astype(jnp.float32), 0.0)
            on = jnp.where(y.astype(jnp.bfloat16) > 0, jnp.bfloat16(1), jnp.bfloat16(0))
            mask_out[j, :, cs] = on
            p_out[:, cs] += y
            n_out[:, cs] += on
        return carry

    lax.fori_loop(0, p_out.shape[1] // wide, chunk, 0)

    @pl.when(step == pl.num_programs(0) - 1)
    def _():
        p_out[...] = p_out[...] * (1.0 / spatial)


def forward_pool(a3, s3, wb, stats):
    spatial, per_dev, c_mid = a3.shape
    c_out = wb.shape[1]
    fixed = lambda shape: pl.BlockSpec(shape, lambda i: (0,) * len(shape))
    part = lambda width: pl.BlockSpec((POS, per_dev, width), lambda i: (i, 0, 0))
    return pl.pallas_call(
        functools.partial(pool_kernel, spatial),
        grid=(spatial // POS,),
        in_specs=[part(c_mid), part(c_out), fixed(wb.shape), fixed(stats.shape)],
        out_specs=[fixed((per_dev, c_out)), fixed((per_dev, c_out)), part(c_out)],
        out_shape=[
            jax.ShapeDtypeStruct((per_dev, c_out), jnp.float32),
            jax.ShapeDtypeStruct((per_dev, c_out), jnp.bfloat16),
            jax.ShapeDtypeStruct((spatial, per_dev, c_out), jnp.bfloat16),
        ],
        compiler_params=pltpu.CompilerParams(dimension_semantics=("arbitrary",), vmem_limit_bytes=VMEM_LIMIT),
        cost_estimate=pl.CostEstimate(flops=2 * spatial * per_dev * c_mid * c_out, bytes_accessed=4 * spatial * per_dev * c_out, transcendentals=0),
        name="forward_pool",
    )(a3, s3, wb, stats)


def head_kernel(classes, global_rows, spatial, tiles, bsum, w_hbm, tail, bias, p, lab, wy, dpool_out, own_out, loss_out, wide_out, pt, wb, zb, acc, wsum, top, tot, ly, ring, sem):
    step = pl.program_id(0)
    rows, feats = p.shape
    width = ring.shape[1]
    now, prev = lax.rem(step, 2), lax.rem(step + 1, 2)
    left = classes - (tiles - 1) * width

    def fetch(i):
        slot = lax.rem(i, RING)
        return pltpu.make_async_copy(w_hbm.at[aligned(i * width, width)], ring.at[slot], sem.at[slot])

    def column(x):
        return jnp.broadcast_to(x, (LANES, rows)).T

    def logits(w):
        wb[now] = w
        b = jnp.broadcast_to(bias[...], (LANES, width)).T
        wide_out[...] = b
        half = width // 2
        for h in range(2):
            at = slice(h * half, (h + 1) * half)
            zb[now, at] = jnp.dot(w[at], pt[...], preferred_element_type=jnp.float32) + tiled(b[at], rows // LANES)

    @pl.when(step == 0)
    def _():
        for i in range(RING - 1):
            fetch(i).start()
        pt[...] = p[...].astype(jnp.bfloat16).T
        acc[...] = jnp.zeros_like(acc)
        wsum[...] = jnp.zeros_like(wsum)
        top[...] = jnp.full_like(top, -1e30)
        tot[...] = jnp.zeros_like(tot)
        ly[...] = jnp.zeros_like(ly)
        row = lax.broadcasted_iota(jnp.int32, (width, feats), 0)
        logits(jnp.where(row < left, tail[...], 0.0).astype(jnp.bfloat16))
        row = lax.broadcasted_iota(jnp.int32, (width, rows), 0)
        zb[now] = jnp.where(row < left, zb[now], -1e30)

    @pl.when(jnp.logical_and(step > 0, step < tiles))
    def _():
        fetch(step - 1).wait()

    @pl.when(jnp.logical_and(step > 0, step + RING - 2 < tiles - 1))
    def _():
        fetch(step + RING - 2).start()

    @pl.when(step > 0)
    def _():
        z = zb[prev]
        old = top[...]
        new = jnp.maximum(old, jnp.max(z, axis=0, keepdims=True))
        corr = jnp.exp(old - new)
        e = jnp.exp(z - new)
        top[...] = new
        tot[...] = tot[...] * corr + jnp.sum(e, axis=0, keepdims=True)
        base = jnp.where(step == 1, tiles - 1, step - 2) * width
        row = lax.broadcasted_iota(jnp.int32, (width, rows), 0) + base
        ly[...] += jnp.sum(jnp.where(lab[...] == row, z, 0.0), axis=0, keepdims=True)
        lead = jnp.concatenate([e.astype(jnp.bfloat16).T, jnp.ones((16, width), jnp.bfloat16)], axis=0)
        wide_corr = column(corr)
        logits(ring[lax.rem(step + RING - 1, RING)].astype(jnp.bfloat16))
        for n in range(feats // CHUNK):
            cs = slice(n * CHUNK, (n + 1) * CHUNK)
            part = jnp.dot(lead, wb[prev, :, cs], preferred_element_type=jnp.float32)
            acc[:, cs] = acc[:, cs] * tiled(wide_corr, CHUNK // LANES) + part[:rows]
            wsum[:, cs] += part[rows:rows + 8]

    @pl.when(step == tiles)
    def _():
        lse = top[...] + jnp.log(tot[...])
        ws = wsum[0:1, :]
        lsum = jnp.sum(pt[...].astype(jnp.float32) * tiled(jnp.broadcast_to(ws, (LANES, feats)).T, rows // LANES), axis=0, keepdims=True) + bsum[0]
        own_out[...] = jnp.concatenate([lse, lab[...].astype(jnp.float32)] + [jnp.zeros_like(lse)] * 6, axis=0)
        loss = lse - (1.0 - SMOOTHING) * ly[...] - SMOOTHING / classes * lsum
        loss_out[...] = jnp.full(loss_out.shape, jnp.sum(loss) * (1.0 / global_rows), jnp.float32)
        d = acc[...] / tiled(column(tot[...]), feats // LANES) - (1.0 - SMOOTHING) * wy[...] - SMOOTHING / classes * ws
        dpool_out[...] = d * (1.0 / (global_rows * spatial))


def head_pass(wt, bias, p, lab, wy, global_rows, spatial):
    classes, feats = wt.shape
    rows = p.shape[0]
    tiles = pl.cdiv(classes, WIDTH)
    fixed = lambda shape: pl.BlockSpec(shape, lambda i: (0,) * len(shape), pipeline_mode=pl.Buffered(1))
    kept = lambda shape: pl.BlockSpec(shape, lambda i: (0,) * len(shape))
    line = (1, rows)
    order = lambda i: jnp.where(i == 0, tiles - 1, jnp.minimum(i - 1, tiles - 2))
    return pl.pallas_call(
        functools.partial(head_kernel, classes, global_rows, spatial, tiles),
        grid=(tiles + 1,),
        in_specs=[
            pl.BlockSpec(memory_space=pltpu.SMEM),
            pl.BlockSpec(memory_space=pl.ANY),
            pl.BlockSpec((WIDTH, feats), lambda i: (tiles - 1, 0), pipeline_mode=pl.Buffered(1)),
            pl.BlockSpec((1, WIDTH), lambda i: (0, order(i))),
            fixed(p.shape), fixed(line), fixed(p.shape),
        ],
        out_specs=[kept(p.shape), kept((8, rows)), kept((8, LANES)), pl.BlockSpec((WIDTH, LANES), lambda i: (order(i), 0))],
        out_shape=[
            jax.ShapeDtypeStruct(p.shape, jnp.float32),
            jax.ShapeDtypeStruct((8, rows), jnp.float32),
            jax.ShapeDtypeStruct((8, LANES), jnp.float32),
            jax.ShapeDtypeStruct((tiles * WIDTH, LANES), jnp.float32),
        ],
        scratch_shapes=[
            pltpu.VMEM((feats, rows), jnp.bfloat16), pltpu.VMEM((2, WIDTH, feats), jnp.bfloat16), pltpu.VMEM((2, WIDTH, rows), jnp.float32),
            pltpu.VMEM(p.shape, jnp.float32), pltpu.VMEM((8, feats), jnp.float32),
        ] + [pltpu.VMEM(line, jnp.float32)] * 3 + [pltpu.VMEM((RING, WIDTH, feats), jnp.float32), pltpu.SemaphoreType.DMA((RING,))],
        compiler_params=pltpu.CompilerParams(dimension_semantics=("arbitrary",), vmem_limit_bytes=VMEM_LIMIT),
        cost_estimate=pl.CostEstimate(flops=4 * rows * feats * classes, bytes_accessed=4 * classes * feats, transcendentals=0),
        name="head_pass",
    )(jnp.sum(bias)[None], wt, wt, bias[None, :], p, lab[None, :], wy)


def conv_grad_kernel(pos_count, a, mask, dpool, n_on, stats, asum, gcw_hbm, wb_hbm, dconv_out, dgamma_out, dbeta_out, db, gcw, wb, sem):
    step = pl.program_id(0)
    c_mid = a.shape[-1]
    c_out = dpool.shape[1]
    late = [pltpu.make_async_copy(gcw_hbm, gcw, sem.at[0]), pltpu.make_async_copy(wb_hbm, wb, sem.at[1])]

    @pl.when(step == 0)
    def _():
        for copy in late:
            copy.start()
        db[...] = dpool[...].astype(jnp.bfloat16)
        dconv_out[...] = jnp.zeros_like(dconv_out)

    x = a[...].reshape(-1, c_mid)
    for n in range(c_out // CHUNK):
        cs = slice(n * CHUNK, (n + 1) * CHUNK)
        d = (mask[:, :, cs] * db[:, cs][None]).reshape(-1, CHUNK)
        dconv_out[:, cs] += lax.dot_general(x, d, (((0,), (0,)), ((), ())), preferred_element_type=jnp.float32)

    @pl.when(step == pl.num_programs(0) - 1)
    def _():
        for copy in late:
            copy.wait()

        def finish(n, carry):
            cs = aligned(n * CHUNK, CHUNK)
            mean, inv, scale = stats[0:1, cs], stats[1:2, cs], stats[2:3, cs]
            count = n_on[:, cs].astype(jnp.float32)
            dbeta_out[:, cs] = jnp.sum(dpool[:, cs] * count, axis=0, keepdims=True)
            dbeta = jnp.sum(db[:, cs].astype(jnp.float32) * count, axis=0, keepdims=True)
            m = dconv_out[:, cs]
            dgamma = inv * (jnp.sum(m * wb[:, cs].astype(jnp.float32), axis=0, keepdims=True) - mean * dbeta)
            dgamma_out[:, cs] = dgamma
            lead = tiled(asum[...], CHUNK // LANES)
            dconv_out[:, cs] = scale * (m - lead * (dbeta / pos_count) - gcw[:, cs] * (inv * dgamma / pos_count))
            return carry

        lax.fori_loop(0, c_out // CHUNK, finish, 0)


def conv_grad(a3, mask, dpool, n_on, stats, gcw, asum, wb):
    spatial, per_dev, c_mid = a3.shape
    c_out = wb.shape[1]
    pos_count = spatial * per_dev
    fixed = lambda a: pl.BlockSpec(a.shape, lambda i: (0, 0), pipeline_mode=pl.Buffered(1))
    part = lambda width: pl.BlockSpec((POS, per_dev, width), lambda i: (i, 0, 0))
    anywhere = pl.BlockSpec(memory_space=pl.ANY)
    kept = lambda rows: pl.BlockSpec((rows, c_out), lambda i: (0, 0))
    return pl.pallas_call(
        functools.partial(conv_grad_kernel, pos_count),
        grid=(spatial // POS,),
        in_specs=[part(c_mid), part(c_out), fixed(dpool), fixed(n_on), fixed(stats), fixed(asum), anywhere, anywhere],
        out_specs=[kept(c_mid), kept(1), kept(1)],
        out_shape=[jax.ShapeDtypeStruct((rows, c_out), jnp.float32) for rows in (c_mid, 1, 1)],
        scratch_shapes=[pltpu.VMEM(dpool.shape, jnp.bfloat16), pltpu.VMEM(gcw.shape, jnp.float32), pltpu.VMEM(wb.shape, jnp.bfloat16), pltpu.SemaphoreType.DMA((2,))],
        compiler_params=pltpu.CompilerParams(dimension_semantics=("arbitrary",), vmem_limit_bytes=VMEM_LIMIT),
        cost_estimate=pl.CostEstimate(flops=2 * pos_count * c_mid * c_out, bytes_accessed=2 * pos_count * c_out, transcendentals=0),
        name="conv_grad",
    )(a3, mask, dpool, n_on, stats, asum, gcw, wb)


def solution(mesh):
    groups = mesh.shape['dp']

    def local_step(act_in, shortcut, labels, w_conv, bn_gamma, bn_beta, w_fc, fc_bias, vel_conv, vel_gamma, vel_beta, vel_fc, vel_bias, learn_rate):
        per_dev = act_in.shape[0]
        global_rows = per_dev * groups
        spatial = act_in.shape[1] * act_in.shape[2]
        c_mid = act_in.shape[3]
        c_out = shortcut.shape[3]
        classes = w_fc.shape[1]
        dev = lax.axis_index('dp')
        wt, vt = w_fc.T, vel_fc.T
        a3 = act_in.reshape(per_dev, spatial, c_mid).transpose(1, 0, 2)
        s3 = shortcut.reshape(per_dev, spatial, c_out).transpose(1, 0, 2)
        gcw, stats, asum, wb = batch_stats(a3, w_conv, bn_gamma, bn_beta)
        pooled, n_on, mask = forward_pool(a3, s3, wb, stats)
        p_all = lax.all_gather(pooled, 'dp', tiled=True)
        wy = wt.at[labels].get(mode='promise_in_bounds')
        d_pool, own, loss_rows, bias_wide = head_pass(wt, fc_bias, pooled, labels, wy, global_rows, spatial)
        d_conv, d_gamma, d_beta = conv_grad(a3, mask, d_pool, n_on, stats, gcw, asum, wb)
        own, p_all, d_conv = lax.optimization_barrier((own, p_all, d_conv))
        lr = learn_rate[None]
        grads, p_bf, db, rows_in, rate = shared_grads(groups, wt, bias_wide, p_all, own, lr)
        n_tiles = pl.cdiv(classes, TILE)
        half = pl.cdiv(n_tiles, 2)
        db = jnp.sum(db[:half, :NORM * BLK], axis=-1) / global_rows
        d_bias = lax.dynamic_update_slice(jnp.zeros((half, 2, TILE), jnp.float32), db[:, None, :], (0, dev % 2, dev // 2 * NORM * BLK))
        vec = jnp.concatenate([d_bias.reshape(-1)[:classes], d_gamma[0], d_beta[0], loss_rows[0, :1]])
        g_conv, vec = lax.psum((d_conv, vec), 'dp')
        fc_new, fc_vel_new, dep = fused_update(rate, wt, vt, grads, bias_wide, p_bf, rows_in)
        conv_new, conv_vel_new = conv_update(dep, lr, g_conv, w_conv, vel_conv)
        g_bias, g_gamma, g_beta, loss_val = vec[:classes], vec[classes:classes + c_out], vec[classes + c_out:classes + 2 * c_out], vec[classes + 2 * c_out]
        gamma_vel_new = MOMENTUM * vel_gamma + learn_rate * g_gamma
        beta_vel_new = MOMENTUM * vel_beta + learn_rate * g_beta
        bias_vel_new = MOMENTUM * vel_bias + learn_rate * g_bias
        return (conv_new, bn_gamma - gamma_vel_new, bn_beta - beta_vel_new, fc_new.T, fc_bias - bias_vel_new, conv_vel_new, gamma_vel_new, beta_vel_new, fc_vel_new.T, bias_vel_new, loss_val)

    return jax.shard_map(local_step, mesh=mesh, in_specs=(P('dp'),) * 3 + (P(),) * 11, out_specs=(P(),) * 11, check_vma=False)
```

time: 2810 us -> 638 us (0.23)
  waiting for transfers between devices: 1860 us -> 0.06 us
  Pallas kernels: 0 us -> 602 us
  other arithmetic: 576 us -> 5.48 us
  matrix products: 297 us -> 0 us
    psum x2 -> x1, waiting for transfers between devices: 1860 us -> 0.01 us  [local_step(): g_conv, vec = lax.psum((d_conv, vec), 'dp')]
    pallas_call x0 -> x7, Pallas kernels: none -> 602 us  [the longest x1 297 us: fused_update(): pl.pallas_call(functools.partial(update_kernel, classes, rows_total), gri...]
    dot_general x5 -> x0, matrix products: 297 us -> none  [the longest x1 70.7 us: forward_backward(): jnp.dot(pooled_bf, fc_bf, preferred_element_type=jnp.float32) + fc_bias]
    sub x3 -> x0, other arithmetic: 296 us -> none  [the longest x2 296 us: lars_update(): return (weight - new_vel, new_vel)]
    reduce_sum x9 -> x2, other arithmetic: 278 us -> 2.42 us  [the longest x1 1.8 us: local_step(): db = jnp.sum(db[:half, :NORM * BLK], axis=-1) / global_rows]
  transfers between devices with their start and end apart: 2 -> 2, of which waited for: 1 -> 0; matrix products, arithmetic and copies ran while one was open for 6% -> 1% of each run, Pallas kernels for 0% -> 65%
where the time goes in v2:
time: 638 us; the launch traced here: 634 us
  Pallas kernels  602 us (94%)
  between operations  14.9 us (2%)
  local copies, waits for them, and re-layouts  10.8 us (2%)
    pallas_call x1, Pallas kernels, fused_update(): pl.pallas_call(functools.partial(update_kernel, classes, rows_total), gri...  297 us
    pallas_call x1, Pallas kernels, shared_grads(): pl.pallas_call(functools.partial(grad_kernel, classes, groups, steps), gr...  111 us
    pallas_call x1, Pallas kernels, head_pass(): pl.pallas_call(functools.partial(head_kernel, classes, global_rows, spati...  76.9 us
    pallas_call x1, Pallas kernels, forward_pool(): pl.pallas_call(functools.partial(pool_kernel, spatial), grid=(spatial //...  52.4 us
    pallas_call x1, Pallas kernels, conv_grad(): pl.pallas_call(functools.partial(conv_grad_kernel, pos_count), grid=(spat...  37.8 us
    pallas_call x1, Pallas kernels, batch_stats(): pl.pallas_call(functools.partial(gram_kernel, pos_count, scans), grid=(sc...  18 us
  transfers between devices with their start and end apart: 2, of which 0 were waited for; matrix products, arithmetic and copies ran while one was open for 1% of the time, Pallas kernels for 65%

profile of v2, /device:TPU:0, one launch (start us, length us, event | category | flops | bytes accessed | tf_op | source)
XLA Modules:
  0.0 633.6 jit_solution(16064701766781102289)
XLA Ops:
  7.2 0.0 all-gather.2.cloned.1.call-start
  7.2 18.0 %batch_stats.1 = (f32[512,2048]{1,0:T(8,128)}, f32[8,2048]{1,0:T(8,128)}, f32[512,128]{1,0:T(8,128)}, bf16[512,2048]{1,0:T(8,128)(2,1)}) custom-call(bf16[49,256,512]{2,1,0:T(8,128)(2,1)} %bitcast.31, f32[512,2048]{1,0:T(8,128)} %w_hbm.1, f32[1,2048]{1,0:T(1,128)} %bitcast.25, f32[1,2048]{1,0:T(1,128)} %bitcast.26), custom_call_target="tpu_custom_call" | custom-call | flops 6576668672 | bytes 12845056 | tf_op jit(solution)/shard_map/batch_stats/pallas_call | solution.py:416
  25.2 0.0 copy-start
  25.2 0.0 copy-start.9
  25.3 52.4 %forward_pool.1 = (f32[256,2048]{1,0:T(8,128)}, bf16[256,2048]{1,0:T(8,128)(2,1)}, bf16[49,256,2048]{2,1,0:T(8,128)(2,1)}) custom-call(bf16[49,256,512]{2,1,0:T(8,128)(2,1)} %bitcast.32, bf16[49,256,2048]{2,1,0:T(8,128)(2,1)} %bitcast.30, bf16[512,2048]{1,0:T(8,128)(2,1)} %get-tuple-element.38.wb.wb_hbm, f32[8,2048]{1,0:T(8,128)} %get-tuple-element.39.stats), custom_call_target="tpu_custom_call" | custom-call | flops 26306674688 | bytes 102760448 | tf_op jit(solution)/shard_map/forward_pool/pallas_call | solution.py:467
  77.7 0.0 all-gather.2.cloned.1.call-update
  77.7 0.2 all-reduce.3.cloned.1.call-start
  78.6 0.0 copy-done
  78.6 0.7 broadcast_in_dim.26.bias
  79.3 0.6 reduce_sum.18
  79.9 0.0 copy-done.9
  79.9 5.2 gather_fusion
  85.1 76.9 %head_pass.1 = (f32[256,2048]{1,0:T(8,128)}, f32[8,256]{1,0:T(8,128)}, f32[8,128]{1,0:T(8,128)}, f32[22016,128]{1,0:T(8,128)}) custom-call(f32[1]{0:T(128)} %bitcast.1.bsum, f32[21843,2048]{1,0:T(8,128)} %bitcast.w_hbm.tail.refs_0_.refs_1_.refs_2_.refs_3_.refs_4_.refs_5_.refs_6_.refs_7_.refs_8_.w_in, ...), custom_call_target="tpu_custom_call" | custom-call | flops 45808091136 | bytes 178937856 | tf_op jit(solution)/shard_map/head_pass/pallas_call | solution.py:570
  162.1 1.2 slice.23
  163.3 37.8 %conv_grad.1 = (f32[512,2048]{1,0:T(8,128)}, f32[1,2048]{1,0:T(1,128)}, f32[1,2048]{1,0:T(1,128)}) custom-call(bf16[49,256,512]{2,1,0:T(8,128)(2,1)} %bitcast.33, bf16[49,256,2048]{2,1,0:T(8,128)(2,1)} %get-tuple-element.43.mask, f32[256,2048]{1,0:T(8,128)} %get-tuple-element.44.dpool, bf16[256,2048]{1,0:T(8,128)(2,1)} %get-tuple-element.45.n_on, ...), custom_call_target="tpu_custom_call" | custom-call | flops 26306674688 | bytes 51380224 | tf_op jit(solution)/shard_map/conv_grad/pallas_call | solution.py:645
  201.0 0.0 all-gather.2.cloned.1.call-done.refs_12_
  201.1 0.0 copy-start.7
  201.1 0.0 copy-start.8
  201.1 110.7 %shared_grads.1 = (f32[2,45,96,2048]{3,2,1,0:T(8,128)}, bf16[2048,2048]{1,0:T(8,128)(2,1)}, f32[45,96,128]{2,1,0:T(8,128)}, f32[8,2048]{1,0:T(8,128)}, f32[8,128]{1,0:T(8,128)}) custom-call(f32[21843,2048]{1,0:T(8,128)} %bitcast.w_hbm.tail.refs_0_.refs_1_.refs_2_.refs_3_.refs_4_.refs_5_.refs_6_.refs_7_.refs_8_.w_in, ...), custom_call_target="tpu_custom_call" | custom-call | flops 72477573120 | bytes 70778880 | tf_op jit(solution)/shard_map/shared_grads/pallas_call | solution.py:210
  311.8 1.8 slice_reduce_fusion
  313.7 0.8 dynamic_update_slice.3
  314.5 0.1 reshape.42
  314.6 0.0 copy-done.7
  314.6 0.0 copy-done.8
  314.6 1.4 concatenate.3
  316.0 0.0 all-reduce.3.cloned.1.call-update
  316.0 0.0 copy-start.1
  316.0 0.0 copy-start.2
  316.1 0.0 copy-start.3
  316.1 0.0 copy-start.4
  316.1 0.0 copy-start.5
  316.1 0.0 copy-start.6
  316.1 297.4 %fused_update.1 = (f32[21843,2048]{1,0:T(8,128)}, f32[21843,2048]{1,0:T(8,128)}, f32[8,128]{1,0:T(8,128)}) custom-call(f32[8,128]{1,0:T(8,128)} %get-tuple-element.51.rate, f32[21843,2048]{1,0:T(8,128)} %bitcast.w_hbm.tail.refs_0_.refs_1_.refs_2_.refs_3_.refs_4_.refs_5_.refs_6_.refs_7_.refs_8_.w_in, f32[21843,2048]{1,0:T(8,128)} %bitcast.11.v_in, ...), custom_call_target="tpu_custom_call" | custom-call | flops 230854492160 | bytes 715751424 | tf_op jit(solution)/shard_map/fused_update/pallas_call | solution.py:293
  613.5 0.0 all-reduce.3.cloned.1.call-done
  613.5 1.3 slice.34
  614.7 0.0 copy-done.1
  614.7 0.0 copy-done.2
  614.7 1.6 fusion.3
  616.3 0.0 copy-done.3
  616.3 0.0 copy-done.4
  616.3 0.0 copy-done.5
  616.3 0.0 copy-done.6
  616.3 1.5 fusion.5
  617.8 8.9 %conv_update.1 = (f32[512,2048]{1,0:T(8,128)}, f32[512,2048]{1,0:T(8,128)}) custom-call(f32[8,128]{1,0:T(8,128)} %get-tuple-element.55.dep, f32[1]{0:T(128)} %bitcast.23.lr, f32[512,2048]{1,0:T(8,128)} %get-tuple-element.65.g_hbm, f32[512,2048]{1,0:T(8,128)} %w_hbm.1, f32[512,2048]{1,0:T(8,128)} %v_hbm.1), custom_call_target="tpu_custom_call" | custom-call | flops 10485760 | bytes 20971520 | tf_op jit(solution)/shard_map/conv_update/pallas_call | solution.py:351
  (5 shorter events, 0.1 us)
Async XLA Ops:
  7.2 193.9 %all-gather.2.cloned.1.call-start = ((), (), s32[]{:S(2)}) async-start(), calls=%async_computation | async-start | bytes 18874368 | tf_op jit(solution)/shard_map/all_gather | solution.py:674
  25.2 53.4 %copy-start = (f32[21843]{0:T(1024)S(1)}, f32[21843]{0:T(1024)}, u32[]{:S(2)}) copy-start(f32[21843]{0:T(1024)} %param.21) | copy-start | bytes 262120
  25.2 54.7 %copy-start.9 = (s32[256]{0:T(256)S(1)}, s32[256]{0:T(256)}, u32[]{:S(2)}) copy-start(s32[256]{0:T(256)} %param.16) | copy-start | bytes 3076
  77.7 535.8 %all-reduce.3.cloned.1.call-start = ((), (), s32[]{:S(2)}) async-start(), calls=%async_computation.1 | async-start | bytes 8601600 | tf_op jit(solution)/shard_map/psum | solution.py:686
  201.1 113.6 %copy-start.7 = (f32[1,2048]{1,0:T(1,128)S(1)}, f32[1,2048]{1,0:T(1,128)}, u32[]{:S(2)}) copy-start(f32[1,2048]{1,0:T(1,128)} %get-tuple-element.59) | copy-start | bytes 24580
  201.1 113.5 %copy-start.8 = (f32[1,2048]{1,0:T(1,128)S(1)}, f32[1,2048]{1,0:T(1,128)}, u32[]{:S(2)}) copy-start(f32[1,2048]{1,0:T(1,128)} %get-tuple-element.60) | copy-start | bytes 24580
  316.0 298.7 %copy-start.1 = (f32[21843]{0:T(1024)S(1)}, f32[21843]{0:T(1024)}, u32[]{:S(2)}) copy-start(f32[21843]{0:T(1024)} %param.21) | copy-start | bytes 262120
  316.0 298.7 %copy-start.2 = (f32[21843]{0:T(1024)S(1)}, f32[21843]{0:T(1024)}, u32[]{:S(2)}) copy-start(f32[21843]{0:T(1024)} %param.26) | copy-start | bytes 262120
  316.1 300.3 %copy-start.3 = (f32[2048]{0:T(1024)S(1)}, f32[2048]{0:T(1024)}, u32[]{:S(2)}) copy-start(f32[2048]{0:T(1024)} %param.18) | copy-start | bytes 24580
  316.1 300.3 %copy-start.4 = (f32[2048]{0:T(1024)S(1)}, f32[2048]{0:T(1024)}, u32[]{:S(2)}) copy-start(f32[2048]{0:T(1024)} %param.19) | copy-start | bytes 24580
  316.1 300.2 %copy-start.5 = (f32[2048]{0:T(1024)S(1)}, f32[2048]{0:T(1024)}, u32[]{:S(2)}) copy-start(f32[2048]{0:T(1024)} %param.24) | copy-start | bytes 24580
  316.1 300.2 %copy-start.6 = (f32[2048]{0:T(1024)S(1)}, f32[2048]{0:T(1024)}, u32[]{:S(2)}) copy-start(f32[2048]{0:T(1024)} %param.23) | copy-start | bytes 24580
Sparse Core Ops, SparseCore 0:
  77.8 86.8 all-gather.1
  316.2 77.2 all-reduce.2

commit v3 on v2

--- a/solution.py
+++ b/solution.py
@@ -25,6 +25,7 @@
 LANES = 128
 SUB = 8
 RING = 4
+DEPTH = 3
 VMEM_LIMIT = 66_000_000
 
 
@@ -91,10 +92,11 @@
 
     @pl.when(step == 0)
     def _():
-        def fetch(i, slot):
-            return pltpu.make_async_copy(p_all.at[aligned(i * per_dev, per_dev)], pbuf.at[slot], p_sem.at[slot])
-
-        fetch(0, 0).start()
+        def fetch(i):
+            return pltpu.make_async_copy(p_all.at[aligned(i * per_dev, per_dev)], pbuf.at[i], p_sem.at[i])
+
+        for i in range(groups):
+            fetch(i).start()
         barrier = pltpu.get_barrier_semaphore()
         for o in range(1, groups):
             pl.semaphore_signal(barrier, 1, device_id=((me + o) % groups,), device_id_type=pl.DeviceIdType.MESH)
@@ -106,12 +108,8 @@
         prepare(0)
 
         def convert(i, carry):
-            @pl.when(i + 1 < groups)
-            def _():
-                fetch(i + 1, (i + 1) % 2).start()
-            fetch(i, i % 2).wait()
-            at = aligned(i * per_dev, per_dev)
-            p[at, :] = pbuf[i % 2].astype(jnp.bfloat16)
+            fetch(i).wait()
+            p[aligned(i * per_dev, per_dev), :] = pbuf[i].astype(jnp.bfloat16)
             return carry
 
         lax.fori_loop(0, groups, convert, 0)
@@ -149,8 +147,14 @@
                 for m in range(CHUNK // LANES):
                     sums[k] = sums[k] + d[:, m * LANES:(m + 1) * LANES]
                 dmat[rs, cs] = d.astype(jnp.bfloat16)
-        for k in range(nw):
-            db_out[k // HAVE, (k % HAVE) * BLK:(k % HAVE + 1) * BLK, :] = sums[k]
+        lane = lax.broadcasted_iota(jnp.int32, (1, TILE), 1)
+        db_out[...] = jnp.zeros_like(db_out)
+        for t in range(GROUP):
+            line = jnp.zeros((1, TILE), jnp.float32)
+            for i in range(NORM):
+                row = jnp.sum(sums[t * HAVE + i].T, axis=0, keepdims=True)
+                line = jnp.where(lane // BLK == slot_of(i), tiled(row, SLOTS), line)
+            db_out[0, pl.ds(2 * t + c, 1), :] = line * (1.0 / rows_total)
         for n in range(feats // CHUNK):
             cs = slice(n * CHUNK, (n + 1) * CHUNK)
             g = jnp.dot(dmat[...], p[:, cs], preferred_element_type=jnp.float32) * (1.0 / rows_total)
@@ -170,13 +174,14 @@
             msg[i] = total
         local(steps - 1).start()
         remote(steps - 1).start()
-        for group in (steps - 2, steps - 1):
-            local(group).wait()
-            remote(group).wait_send()
         keep.wait()
+        local(steps - 2).wait()
+        remote(steps - 2).wait_send()
         for copy in spread(msg, msgs, msg_s, msg_r):
             copy.start()
         msgs[me] = msg[...]
+        local(steps - 1).wait()
+        remote(steps - 1).wait_send()
         for group in range(steps):
             arrival(group).wait_recv()
         for copy in spread(msg, msgs, msg_s, msg_r):
@@ -215,25 +220,25 @@
         + [anywhere, pl.BlockSpec(own.shape, lambda s: (0, 0)), pl.BlockSpec(memory_space=pltpu.SMEM)],
         out_specs=[
             anywhere, anywhere,
-            pl.BlockSpec((GROUP, HAVE * BLK, LANES), lambda s: (jnp.maximum(s - 1, 0), 0, 0)),
+            pl.BlockSpec((1, 2 * GROUP, TILE), lambda s: (jnp.maximum(s - 1, 0), 0, 0)),
             pl.BlockSpec((8, rows_total), lambda s: (0, 0)),
             pl.BlockSpec((8, LANES), lambda s: (0, 0)),
         ],
         out_shape=[
             jax.ShapeDtypeStruct((2, steps * GROUP, HAVE * BLK, feats), jnp.float32),
             jax.ShapeDtypeStruct((rows_total, feats), jnp.bfloat16),
-            jax.ShapeDtypeStruct((steps * GROUP, HAVE * BLK, LANES), jnp.float32),
+            jax.ShapeDtypeStruct((steps, 2 * GROUP, TILE), jnp.float32),
             jax.ShapeDtypeStruct((8, rows_total), jnp.float32),
             jax.ShapeDtypeStruct((8, LANES), jnp.float32),
         ],
         scratch_shapes=[
             pltpu.VMEM((rows_total, feats), jnp.bfloat16),
-            pltpu.VMEM((2, rows_total // groups, feats), jnp.float32),
+            pltpu.VMEM((groups, rows_total // groups, feats), jnp.float32),
             pltpu.VMEM((2, rows, feats), jnp.bfloat16), pltpu.VMEM((rows, rows_total), jnp.bfloat16),
             pltpu.VMEM((2, GROUP, HAVE * BLK, feats), jnp.float32),
             pltpu.VMEM((groups,) + own.shape, jnp.float32),
             pltpu.VMEM((2, 8, feats), jnp.float32), pltpu.VMEM((2, 8, LANES), jnp.float32), pltpu.VMEM((groups, 2, 8, LANES), jnp.float32),
-            dma((2,)), dma, dma((2,)), dma((2,)), dma((steps,)),
+            dma((groups,)), dma, dma((2,)), dma((2,)), dma((steps,)),
             dma((groups,)), dma((groups,)), dma((groups,)), dma((groups,)),
         ],
         compiler_params=pltpu.CompilerParams(dimension_semantics=("arbitrary",), vmem_limit_bytes=VMEM_LIMIT, collective_id=0, has_side_effects=True),
@@ -242,19 +247,44 @@
     )(*([wt] * (GROUP * HAVE)), *([bias] * GROUP), p_all, own, lr)
 
 
-def update_kernel(classes, rows_total, rate, w_in, v_in, even, odd, bias, p, rows_in, w_out, v_out, done, lhs, dmat):
+def update_kernel(classes, steps, rate, w_hbm, v_hbm, w_end, v_end, even, odd, bias, p, rows_in, w_out, v_out, done, wbuf, vbuf, lhs, dmat, w_sem, v_sem):
     q = lax.axis_index('dp') // 2
     step = pl.program_id(0)
     a = tiled(rate[0:1, :], CHUNK // LANES)
     cols, feats = p.shape
+    tall = 2 * TILE
+    whole = (classes - (steps - 1) * tall) // SUB * SUB
     done[...] = jnp.zeros_like(done)
 
-    def rows_at(base):
-        return aligned(base, BLK)
+    def fetch(i, act, hbm, buf, sem):
+        slot = lax.rem(i, DEPTH)
+
+        def go(size):
+            act(pltpu.make_async_copy(hbm.at[pl.ds(pl.multiple_of(i * tall, tall), size)], buf.at[slot, pl.ds(0, size)], sem.at[slot]))
+
+        @pl.when(i < steps - 1)
+        def _():
+            go(tall)
+
+        @pl.when(i == steps - 1)
+        def _():
+            go(whole)
+
+    start = lambda copy: copy.start()
+    wait = lambda copy: copy.wait()
+
+    def arrived(i, hbm, buf, sem, end):
+        fetch(i, wait, hbm, buf, sem)
+
+        @pl.when(i == steps - 1)
+        def _():
+            buf[lax.rem(i, DEPTH), whole:whole + SUB, :] = end[...]
+
+    slot = lax.rem(step, DEPTH)
 
     def apply(rs, cs, g):
-        w = w_in[rs, cs]
-        nv = MOMENTUM * v_in[rs, cs] + a * (g + WEIGHT_DECAY * w)
+        w = wbuf[slot, rs, cs]
+        nv = MOMENTUM * vbuf[slot, rs, cs] + a * (g + WEIGHT_DECAY * w)
         v_out[rs, cs] = nv
         w_out[rs, cs] = w - nv
 
@@ -262,45 +292,62 @@
     for t in range(2):
         for i in range(HAVE, SLOTS):
             bases.append(t * TILE + (2 * q + i) % SLOTS * BLK)
+
+    @pl.when(step == 0)
+    def _():
+        for i in range(2):
+            fetch(i, start, w_hbm, wbuf, w_sem)
+            fetch(i, start, v_hbm, vbuf, v_sem)
+
+    arrived(step, w_hbm, wbuf, w_sem, w_end)
+    arrived(step, v_hbm, vbuf, v_sem, v_end)
+    fetch(step + 2, start, w_hbm, wbuf, w_sem)
+    fetch(step + 2, start, v_hbm, vbuf, v_sem)
     for k, base in enumerate(bases):
-        lhs[k * BLK:(k + 1) * BLK, :] = w_in[rows_at(base), :].astype(jnp.bfloat16)
+        lhs[k * BLK:(k + 1) * BLK, :] = wbuf[slot, aligned(base, BLK), :].astype(jnp.bfloat16)
     for n in range(cols // CHUNK):
         cs = slice(n * CHUNK, (n + 1) * CHUNK)
         z = lax.dot_general(lhs[...], p[cs, :], (((1,), (1,)), ((), ())), preferred_element_type=jnp.float32)
         for t, src in enumerate((even, odd)):
             for i in range(HAVE):
-                apply(rows_at(t * TILE + (2 * q + i) % SLOTS * BLK), cs, src[0, 0, i * BLK:(i + 1) * BLK, cs])
+                apply(aligned(t * TILE + (2 * q + i) % SLOTS * BLK, BLK), cs, src[0, 0, i * BLK:(i + 1) * BLK, cs])
         for k, base in enumerate(bases):
             rs = slice(k * BLK, (k + 1) * BLK)
-            d = logit_grads(z[rs], bias[rows_at(base), :], rows_in[0:1, cs], rows_in[1:2, cs], step * 2 * TILE + base, classes)
+            d = logit_grads(z[rs], bias[aligned(base, BLK), :], rows_in[0:1, cs], rows_in[1:2, cs], step * tall + base, classes)
             dmat[rs, cs] = d.astype(jnp.bfloat16)
+
     for n in range(feats // CHUNK):
         cs = slice(n * CHUNK, (n + 1) * CHUNK)
-        g = jnp.dot(dmat[...], p[:, cs], preferred_element_type=jnp.float32) * (1.0 / rows_total)
+        g = jnp.dot(dmat[...], p[:, cs], preferred_element_type=jnp.float32) * (1.0 / cols)
         for k, base in enumerate(bases):
-            apply(rows_at(base), cs, g[k * BLK:(k + 1) * BLK])
+            apply(aligned(base, BLK), cs, g[k * BLK:(k + 1) * BLK])
 
 
 def fused_update(rate, wt, vt, grads, bias, p, rows_in):
     classes, feats = wt.shape
-    rows_total = p.shape[0]
-    steps = pl.cdiv(classes, 2 * TILE)
-    once = dict(pipeline_mode=pl.Buffered(1))
-    whole = lambda a: pl.BlockSpec(a.shape, lambda s: (0, 0), **once)
-    tile = pl.BlockSpec((2 * TILE, feats), lambda s: (s, 0))
+    tall = 2 * TILE
+    steps = pl.cdiv(classes, tall)
+    whole = lambda a: pl.BlockSpec(a.shape, lambda s: (0, 0), pipeline_mode=pl.Buffered(1))
+    anywhere = pl.BlockSpec(memory_space=pl.ANY)
+    end = pl.BlockSpec((SUB, feats), lambda s: (classes // SUB, 0), pipeline_mode=pl.Buffered(1))
+    tile = pl.BlockSpec((tall, feats), lambda s: (s, 0))
     part = lambda par: pl.BlockSpec((1, 1, HAVE * BLK, feats), lambda s: (par, s, 0, 0))
     rows = 2 * (SLOTS - HAVE) * BLK
+    dma = pltpu.SemaphoreType.DMA
     return pl.pallas_call(
-        functools.partial(update_kernel, classes, rows_total),
+        functools.partial(update_kernel, classes, steps),
         grid=(steps,),
-        in_specs=[whole(rate), tile, tile, part(0), part(1), pl.BlockSpec((2 * TILE, LANES), lambda s: (s, 0)), whole(p), whole(rows_in)],
-        out_specs=[tile, tile, pl.BlockSpec((8, LANES), lambda s: (0, 0))],
-        scratch_shapes=[pltpu.VMEM((rows, feats), jnp.bfloat16), pltpu.VMEM((rows, rows_total), jnp.bfloat16)],
-        out_shape=[jax.ShapeDtypeStruct(wt.shape, jnp.float32)] * 2 + [jax.ShapeDtypeStruct((8, LANES), jnp.float32)],
+        in_specs=[whole(rate), anywhere, anywhere, end, end, part(0), part(1), pl.BlockSpec((tall, LANES), lambda s: (s, 0)), whole(p), whole(rows_in)],
+        out_specs=[tile, tile, pl.BlockSpec((SUB, LANES), lambda s: (0, 0))],
+        scratch_shapes=[
+            pltpu.VMEM((DEPTH, tall, feats), jnp.float32), pltpu.VMEM((DEPTH, tall, feats), jnp.float32),
+            pltpu.VMEM((rows, feats), jnp.bfloat16), pltpu.VMEM((rows, p.shape[0]), jnp.bfloat16), dma((DEPTH,)), dma((DEPTH,)),
+        ],
+        out_shape=[jax.ShapeDtypeStruct(wt.shape, jnp.float32)] * 2 + [jax.ShapeDtypeStruct((SUB, LANES), jnp.float32)],
         compiler_params=pltpu.CompilerParams(dimension_semantics=("arbitrary",), vmem_limit_bytes=VMEM_LIMIT),
-        cost_estimate=pl.CostEstimate(flops=4 * steps * rows * feats * rows_total, bytes_accessed=16 * classes * feats, transcendentals=0),
+        cost_estimate=pl.CostEstimate(flops=4 * steps * rows * feats * p.shape[0], bytes_accessed=16 * classes * feats, transcendentals=0),
         name="fused_update",
-    )(rate, wt, vt, grads, grads, bias, p, rows_in)
+    )(rate, wt, vt, wt, vt, grads, grads, bias, p, rows_in)
 
 
 def conv_update_kernel(dep, lr, g_hbm, w_hbm, v_hbm, w_out, v_out, g, w, v, sem, out_sem):
@@ -360,19 +407,29 @@
     )(dep, lr, g, w, v)
 
 
-def gram_kernel(pos_count, scans, a, wc, gamma, beta, gcw_out, stats_out, asum_out, wb_out, gram, asum, parts):
+def front_kernel(spatial, scans, chunks, a_hbm, s, wc, gamma, beta, gcw_out, stats_out, asum_out, wb_out, p_out, y_out, a, gram, asum, parts, wb, stats, sem):
     step = pl.program_id(0)
     c_mid = a.shape[-1]
     cols = wc.shape[1]
+    pos_count = spatial * a.shape[1]
+    wide = 2 * CHUNK
+
+    def fetch(i):
+        at = pl.ds(i * POS, POS)
+        return pltpu.make_async_copy(a_hbm.at[at], a.at[at], sem.at[i])
 
     @pl.when(step == 0)
     def _():
+        for i in range(scans):
+            fetch(i).start()
         gram[...] = jnp.zeros_like(gram)
         asum[...] = jnp.zeros_like(asum)
+        p_out[...] = jnp.zeros_like(p_out)
 
     @pl.when(step < scans)
     def _():
-        x = a[...].reshape(-1, c_mid)
+        fetch(step).wait()
+        x = a[pl.ds(step * POS, POS)].reshape(-1, c_mid)
         gram[...] += lax.dot_general(x, x, (((0,), (0,)), ((), ())), preferred_element_type=jnp.float32)
         asum[...] += jnp.sum(x.astype(jnp.float32).reshape(-1, SUB, c_mid), axis=0)
 
@@ -387,100 +444,79 @@
             parts[i] = part
             rest = rest - part.astype(jnp.float32)
 
-    @pl.when(step >= scans)
-    def _():
-        wb = wc[...].astype(jnp.bfloat16)
-        wb_out[...] = wb
-        wr = wb.astype(jnp.float32)
+    @pl.when(jnp.logical_and(step >= scans, step < scans + chunks))
+    def _():
+        at = aligned((step - scans) * cols, cols)
+        w = wc[...].astype(jnp.bfloat16)
+        wb_out[...] = w
+        wb[:, at] = w
+        wr = w.astype(jnp.float32)
         gcw = jnp.zeros((c_mid, cols), jnp.float32)
         for i in reversed(range(parts.shape[0])):
-            gcw = gcw + jnp.dot(parts[i], wb, preferred_element_type=jnp.float32)
+            gcw = gcw + jnp.dot(parts[i], w, preferred_element_type=jnp.float32)
         gcw_out[...] = gcw
         var = jnp.maximum(jnp.sum(wr * gcw, axis=0, keepdims=True) / pos_count, 0.0)
         mean = jnp.sum(wr * tiled(asum_out[...], cols // LANES), axis=0, keepdims=True) / pos_count
         inv = lax.rsqrt(var + BN_EPS)
         scale = gamma[...] * inv
-        stats_out[...] = stack_rows(mean, inv, scale, beta[...] - mean * scale)
-
-
-def stack_rows(*rows):
-    return jnp.concatenate(rows + (jnp.zeros_like(rows[0]),) * (SUB - len(rows)), axis=0)
-
-
-def batch_stats(a3, w_conv, gamma, beta):
+        rows = (mean, inv, scale, beta[...] - mean * scale)
+        rows = jnp.concatenate(rows + (jnp.zeros_like(inv),) * (SUB - len(rows)), axis=0)
+        stats_out[...] = rows
+        stats[:, at] = rows
+
+    @pl.when(step >= scans + chunks)
+    def _():
+        first = (step - scans - chunks) * POS
+
+        def chunk(n, carry):
+            cs = aligned(n * wide, wide)
+            scale, shift = stats[2:3, cs], stats[3:4, cs]
+            for j in range(POS):
+                z = jnp.dot(a[first + j], wb[:, cs], preferred_element_type=jnp.float32)
+                y = jnp.maximum(z * scale + shift + s[j, :, cs].astype(jnp.float32), 0.0)
+                y_out[j, :, cs] = y.astype(jnp.bfloat16)
+                p_out[:, cs] += y
+            return carry
+
+        lax.fori_loop(0, p_out.shape[1] // wide, chunk, 0)
+
+    @pl.when(step == pl.num_programs(0) - 1)
+    def _():
+        p_out[...] = p_out[...] * (1.0 / spatial)
+
+
+def front(a3, s3, w_conv, gamma, beta):
     spatial, per_dev, c_mid = a3.shape
     c_out = w_conv.shape[1]
-    pos_count = spatial * per_dev
-    scans = spatial // POS
-    chunk = lambda rows: pl.BlockSpec((rows, CHUNK), lambda i: (0, jnp.maximum(i - scans, 0)))
+    scans, chunks = spatial // POS, c_out // CHUNK
+    fixed = lambda shape: pl.BlockSpec(shape, lambda i: (0, 0))
+    chunk = lambda rows: pl.BlockSpec((rows, CHUNK), lambda i: (0, jnp.clip(i - scans, 0, chunks - 1)))
+    part = pl.BlockSpec((POS, per_dev, c_out), lambda i: (jnp.maximum(i - scans - chunks, 0), 0, 0))
     return pl.pallas_call(
-        functools.partial(gram_kernel, pos_count, scans),
-        grid=(scans + c_out // CHUNK,),
-        in_specs=[pl.BlockSpec((POS, per_dev, c_mid), lambda i: (jnp.minimum(i, scans - 1), 0, 0)), chunk(c_mid), chunk(1), chunk(1)],
-        out_specs=[chunk(c_mid), chunk(SUB), pl.BlockSpec((c_mid, LANES), lambda i: (0, 0)), chunk(c_mid)],
+        functools.partial(front_kernel, spatial, scans, chunks),
+        grid=(2 * scans + chunks,),
+        in_specs=[pl.BlockSpec(memory_space=pl.ANY), part, chunk(c_mid), chunk(1), chunk(1)],
+        out_specs=[chunk(c_mid), chunk(SUB), fixed((c_mid, LANES)), chunk(c_mid), fixed((per_dev, c_out)), part],
         out_shape=[
             jax.ShapeDtypeStruct((c_mid, c_out), jnp.float32),
             jax.ShapeDtypeStruct((SUB, c_out), jnp.float32),
             jax.ShapeDtypeStruct((c_mid, LANES), jnp.float32),
             jax.ShapeDtypeStruct((c_mid, c_out), jnp.bfloat16),
-        ],
-        scratch_shapes=[pltpu.VMEM((c_mid, c_mid), jnp.float32), pltpu.VMEM((SUB, c_mid), jnp.float32), pltpu.VMEM((3, c_mid, c_mid), jnp.bfloat16)],
-        compiler_params=pltpu.CompilerParams(dimension_semantics=("arbitrary",), vmem_limit_bytes=VMEM_LIMIT),
-        cost_estimate=pl.CostEstimate(flops=2 * pos_count * c_mid * c_mid, bytes_accessed=2 * pos_count * c_mid, transcendentals=0),
-        name="batch_stats",
-    )(a3, w_conv, gamma[None, :], beta[None, :])
-
-
-def pool_kernel(spatial, a, s, wb, stats, p_out, n_out, mask_out):
-    step = pl.program_id(0)
-    wide = 2 * CHUNK
-
-    @pl.when(step == 0)
-    def _():
-        p_out[...] = jnp.zeros_like(p_out)
-        n_out[...] = jnp.zeros_like(n_out)
-
-    def chunk(n, carry):
-        cs = aligned(n * wide, wide)
-        scale, shift = stats[2:3, cs], stats[3:4, cs]
-        for j in range(POS):
-            z = jnp.dot(a[j], wb[:, cs], preferred_element_type=jnp.float32)
-            y = jnp.maximum(z * scale + shift + s[j, :, cs].astype(jnp.float32), 0.0)
-            on = jnp.where(y.astype(jnp.bfloat16) > 0, jnp.bfloat16(1), jnp.bfloat16(0))
-            mask_out[j, :, cs] = on
-            p_out[:, cs] += y
-            n_out[:, cs] += on
-        return carry
-
-    lax.fori_loop(0, p_out.shape[1] // wide, chunk, 0)
-
-    @pl.when(step == pl.num_programs(0) - 1)
-    def _():
-        p_out[...] = p_out[...] * (1.0 / spatial)
-
-
-def forward_pool(a3, s3, wb, stats):
-    spatial, per_dev, c_mid = a3.shape
-    c_out = wb.shape[1]
-    fixed = lambda shape: pl.BlockSpec(shape, lambda i: (0,) * len(shape))
-    part = lambda width: pl.BlockSpec((POS, per_dev, width), lambda i: (i, 0, 0))
-    return pl.pallas_call(
-        functools.partial(pool_kernel, spatial),
-        grid=(spatial // POS,),
-        in_specs=[part(c_mid), part(c_out), fixed(wb.shape), fixed(stats.shape)],
-        out_specs=[fixed((per_dev, c_out)), fixed((per_dev, c_out)), part(c_out)],
-        out_shape=[
             jax.ShapeDtypeStruct((per_dev, c_out), jnp.float32),
-            jax.ShapeDtypeStruct((per_dev, c_out), jnp.bfloat16),
             jax.ShapeDtypeStruct((spatial, per_dev, c_out), jnp.bfloat16),
         ],
+        scratch_shapes=[
+            pltpu.VMEM(a3.shape, jnp.bfloat16), pltpu.VMEM((c_mid, c_mid), jnp.float32), pltpu.VMEM((SUB, c_mid), jnp.float32),
+            pltpu.VMEM((3, c_mid, c_mid), jnp.bfloat16), pltpu.VMEM((c_mid, c_out), jnp.bfloat16), pltpu.VMEM((SUB, c_out), jnp.float32),
+            pltpu.SemaphoreType.DMA((scans,)),
+        ],
         compiler_params=pltpu.CompilerParams(dimension_semantics=("arbitrary",), vmem_limit_bytes=VMEM_LIMIT),
-        cost_estimate=pl.CostEstimate(flops=2 * spatial * per_dev * c_mid * c_out, bytes_accessed=4 * spatial * per_dev * c_out, transcendentals=0),
-        name="forward_pool",
-    )(a3, s3, wb, stats)
-
-
-def head_kernel(classes, global_rows, spatial, tiles, bsum, w_hbm, tail, bias, p, lab, wy, dpool_out, own_out, loss_out, wide_out, pt, wb, zb, acc, wsum, top, tot, ly, ring, sem):
+        cost_estimate=pl.CostEstimate(flops=2 * spatial * per_dev * c_mid * (c_mid + c_out), bytes_accessed=4 * spatial * per_dev * c_out, transcendentals=0),
+        name="front",
+    )(a3, s3, w_conv, gamma[None, :], beta[None, :])
+
+
+def head_kernel(classes, global_rows, spatial, tiles, bsum, lab_s, w_hbm, tail, bias, p, lab, dpool_out, own_out, loss_out, wide_out, pt, wb, zb, acc, wsum, top, tot, ly, ring, wy, sem, row_sem):
     step = pl.program_id(0)
     rows, feats = p.shape
     width = ring.shape[1]
@@ -490,6 +526,9 @@
     def fetch(i):
         slot = lax.rem(i, RING)
         return pltpu.make_async_copy(w_hbm.at[aligned(i * width, width)], ring.at[slot], sem.at[slot])
+
+    def pick(i):
+        return pltpu.make_async_copy(w_hbm.at[pl.ds(lab_s[i], 1)], wy.at[pl.ds(i, 1)], row_sem)
 
     def column(x):
         return jnp.broadcast_to(x, (LANES, rows)).T
@@ -507,6 +546,12 @@
     def _():
         for i in range(RING - 1):
             fetch(i).start()
+
+        def begin(i, carry):
+            pick(i).start()
+            return carry
+
+        lax.fori_loop(0, rows, begin, 0)
         pt[...] = p[...].astype(jnp.bfloat16).T
         acc[...] = jnp.zeros_like(acc)
         wsum[...] = jnp.zeros_like(wsum)
@@ -549,17 +594,18 @@
 
     @pl.when(step == tiles)
     def _():
+        pltpu.make_async_copy(w_hbm.at[pl.ds(0, rows)], wy, row_sem).wait()
         lse = top[...] + jnp.log(tot[...])
         ws = wsum[0:1, :]
         lsum = jnp.sum(pt[...].astype(jnp.float32) * tiled(jnp.broadcast_to(ws, (LANES, feats)).T, rows // LANES), axis=0, keepdims=True) + bsum[0]
         own_out[...] = jnp.concatenate([lse, lab[...].astype(jnp.float32)] + [jnp.zeros_like(lse)] * 6, axis=0)
         loss = lse - (1.0 - SMOOTHING) * ly[...] - SMOOTHING / classes * lsum
-        loss_out[...] = jnp.full(loss_out.shape, jnp.sum(loss) * (1.0 / global_rows), jnp.float32)
+        loss_out[0] = jnp.sum(loss) * (1.0 / global_rows)
         d = acc[...] / tiled(column(tot[...]), feats // LANES) - (1.0 - SMOOTHING) * wy[...] - SMOOTHING / classes * ws
         dpool_out[...] = d * (1.0 / (global_rows * spatial))
 
 
-def head_pass(wt, bias, p, lab, wy, global_rows, spatial):
+def head_pass(wt, bias, p, lab, global_rows, spatial):
     classes, feats = wt.shape
     rows = p.shape[0]
     tiles = pl.cdiv(classes, WIDTH)
@@ -572,29 +618,30 @@
         grid=(tiles + 1,),
         in_specs=[
             pl.BlockSpec(memory_space=pltpu.SMEM),
+            pl.BlockSpec(memory_space=pltpu.SMEM),
             pl.BlockSpec(memory_space=pl.ANY),
             pl.BlockSpec((WIDTH, feats), lambda i: (tiles - 1, 0), pipeline_mode=pl.Buffered(1)),
             pl.BlockSpec((1, WIDTH), lambda i: (0, order(i))),
-            fixed(p.shape), fixed(line), fixed(p.shape),
+            fixed(p.shape), fixed(line),
         ],
-        out_specs=[kept(p.shape), kept((8, rows)), kept((8, LANES)), pl.BlockSpec((WIDTH, LANES), lambda i: (order(i), 0))],
+        out_specs=[kept(p.shape), kept((8, rows)), pl.BlockSpec(memory_space=pltpu.SMEM), pl.BlockSpec((WIDTH, LANES), lambda i: (order(i), 0))],
         out_shape=[
             jax.ShapeDtypeStruct(p.shape, jnp.float32),
             jax.ShapeDtypeStruct((8, rows), jnp.float32),
-            jax.ShapeDtypeStruct((8, LANES), jnp.float32),
+            jax.ShapeDtypeStruct((1,), jnp.float32),
             jax.ShapeDtypeStruct((tiles * WIDTH, LANES), jnp.float32),
         ],
         scratch_shapes=[
             pltpu.VMEM((feats, rows), jnp.bfloat16), pltpu.VMEM((2, WIDTH, feats), jnp.bfloat16), pltpu.VMEM((2, WIDTH, rows), jnp.float32),
             pltpu.VMEM(p.shape, jnp.float32), pltpu.VMEM((8, feats), jnp.float32),
-        ] + [pltpu.VMEM(line, jnp.float32)] * 3 + [pltpu.VMEM((RING, WIDTH, feats), jnp.float32), pltpu.SemaphoreType.DMA((RING,))],
+        ] + [pltpu.VMEM(line, jnp.float32)] * 3 + [pltpu.VMEM((RING, WIDTH, feats), jnp.float32), pltpu.VMEM(p.shape, jnp.float32), pltpu.SemaphoreType.DMA((RING,)), pltpu.SemaphoreType.DMA],
         compiler_params=pltpu.CompilerParams(dimension_semantics=("arbitrary",), vmem_limit_bytes=VMEM_LIMIT),
         cost_estimate=pl.CostEstimate(flops=4 * rows * feats * classes, bytes_accessed=4 * classes * feats, transcendentals=0),
         name="head_pass",
-    )(jnp.sum(bias)[None], wt, wt, bias[None, :], p, lab[None, :], wy)
-
-
-def conv_grad_kernel(pos_count, a, mask, dpool, n_on, stats, asum, gcw_hbm, wb_hbm, dconv_out, dgamma_out, dbeta_out, db, gcw, wb, sem):
+    )(jnp.sum(bias)[None], lab, wt, wt, bias[None, :], p, lab[None, :])
+
+
+def conv_grad_kernel(pos_count, a, y, dpool, stats, asum, gcw_hbm, wb_hbm, dconv_out, dgamma_out, dbeta_out, db, n_on, gcw, wb, sem):
     step = pl.program_id(0)
     c_mid = a.shape[-1]
     c_out = dpool.shape[1]
@@ -606,11 +653,18 @@
             copy.start()
         db[...] = dpool[...].astype(jnp.bfloat16)
         dconv_out[...] = jnp.zeros_like(dconv_out)
+        n_on[...] = jnp.zeros_like(n_on)
 
     x = a[...].reshape(-1, c_mid)
     for n in range(c_out // CHUNK):
         cs = slice(n * CHUNK, (n + 1) * CHUNK)
-        d = (mask[:, :, cs] * db[:, cs][None]).reshape(-1, CHUNK)
+        on = y[:, :, cs] > 0
+        ones = jnp.where(on, jnp.bfloat16(1), jnp.bfloat16(0))
+        count = ones[0]
+        for j in range(1, POS):
+            count = count + ones[j]
+        n_on[:, cs] += count
+        d = (ones * db[:, cs][None]).reshape(-1, CHUNK)
         dconv_out[:, cs] += lax.dot_general(x, d, (((0,), (0,)), ((), ())), preferred_element_type=jnp.float32)
 
     @pl.when(step == pl.num_programs(0) - 1)
@@ -634,7 +688,7 @@
         lax.fori_loop(0, c_out // CHUNK, finish, 0)
 
 
-def conv_grad(a3, mask, dpool, n_on, stats, gcw, asum, wb):
+def conv_grad(a3, y, dpool, stats, gcw, asum, wb):
     spatial, per_dev, c_mid = a3.shape
     c_out = wb.shape[1]
     pos_count = spatial * per_dev
@@ -645,14 +699,14 @@
     return pl.pallas_call(
         functools.partial(conv_grad_kernel, pos_count),
         grid=(spatial // POS,),
-        in_specs=[part(c_mid), part(c_out), fixed(dpool), fixed(n_on), fixed(stats), fixed(asum), anywhere, anywhere],
+        in_specs=[part(c_mid), part(c_out), fixed(dpool), fixed(stats), fixed(asum), anywhere, anywhere],
         out_specs=[kept(c_mid), kept(1), kept(1)],
         out_shape=[jax.ShapeDtypeStruct((rows, c_out), jnp.float32) for rows in (c_mid, 1, 1)],
-        scratch_shapes=[pltpu.VMEM(dpool.shape, jnp.bfloat16), pltpu.VMEM(gcw.shape, jnp.float32), pltpu.VMEM(wb.shape, jnp.bfloat16), pltpu.SemaphoreType.DMA((2,))],
+        scratch_shapes=[pltpu.VMEM(dpool.shape, jnp.bfloat16), pltpu.VMEM(dpool.shape, jnp.bfloat16), pltpu.VMEM(gcw.shape, jnp.float32), pltpu.VMEM(wb.shape, jnp.bfloat16), pltpu.SemaphoreType.DMA((2,))],
         compiler_params=pltpu.CompilerParams(dimension_semantics=("arbitrary",), vmem_limit_bytes=VMEM_LIMIT),
         cost_estimate=pl.CostEstimate(flops=2 * pos_count * c_mid * c_out, bytes_accessed=2 * pos_count * c_out, transcendentals=0),
         name="conv_grad",
-    )(a3, mask, dpool, n_on, stats, asum, gcw, wb)
+    )(a3, y, dpool, stats, asum, gcw, wb)
 
 
 def solution(mesh):
@@ -669,20 +723,14 @@
         wt, vt = w_fc.T, vel_fc.T
         a3 = act_in.reshape(per_dev, spatial, c_mid).transpose(1, 0, 2)
         s3 = shortcut.reshape(per_dev, spatial, c_out).transpose(1, 0, 2)
-        gcw, stats, asum, wb = batch_stats(a3, w_conv, bn_gamma, bn_beta)
-        pooled, n_on, mask = forward_pool(a3, s3, wb, stats)
+        gcw, stats, asum, wb, pooled, y = front(a3, s3, w_conv, bn_gamma, bn_beta)
         p_all = lax.all_gather(pooled, 'dp', tiled=True)
-        wy = wt.at[labels].get(mode='promise_in_bounds')
-        d_pool, own, loss_rows, bias_wide = head_pass(wt, fc_bias, pooled, labels, wy, global_rows, spatial)
-        d_conv, d_gamma, d_beta = conv_grad(a3, mask, d_pool, n_on, stats, gcw, asum, wb)
+        d_pool, own, loss_part, bias_wide = head_pass(wt, fc_bias, pooled, labels, global_rows, spatial)
+        d_conv, d_gamma, d_beta = conv_grad(a3, y, d_pool, stats, gcw, asum, wb)
         own, p_all, d_conv = lax.optimization_barrier((own, p_all, d_conv))
         lr = learn_rate[None]
         grads, p_bf, db, rows_in, rate = shared_grads(groups, wt, bias_wide, p_all, own, lr)
-        n_tiles = pl.cdiv(classes, TILE)
-        half = pl.cdiv(n_tiles, 2)
-        db = jnp.sum(db[:half, :NORM * BLK], axis=-1) / global_rows
-        d_bias = lax.dynamic_update_slice(jnp.zeros((half, 2, TILE), jnp.float32), db[:, None, :], (0, dev % 2, dev // 2 * NORM * BLK))
-        vec = jnp.concatenate([d_bias.reshape(-1)[:classes], d_gamma[0], d_beta[0], loss_rows[0, :1]])
+        vec = jnp.concatenate([db.reshape(-1)[:classes], d_gamma[0], d_beta[0], loss_part])
         g_conv, vec = lax.psum((d_conv, vec), 'dp')
         fc_new, fc_vel_new, dep = fused_update(rate, wt, vt, grads, bias_wide, p_bf, rows_in)
         conv_new, conv_vel_new = conv_update(dep, lr, g_conv, w_conv, vel_conv)

time: 638 us -> 599 us (0.939)
  Pallas kernels: 602 us -> 575 us
  local copies, waits for them, and re-layouts: 10.8 us -> 4.31 us
    pallas_call x3 -> x2, Pallas kernels: 368 us -> 346 us  [the longest x1 283 us: fused_update(): pl.pallas_call(functools.partial(update_kernel, classes, steps), grid=(st...]
    pallas_call x1, Pallas kernels: 111 us -> 104 us  [shared_grads(): pl.pallas_call(functools.partial(grad_kernel, classes, groups, steps), gr...]
  transfers between devices with their start and end apart: 2 -> 2, of which waited for: 0 -> 0; matrix products, arithmetic and copies ran while one was open for 1% -> 0% of each run, Pallas kernels for 65% -> 67%
where the time goes in v3:
time: 599 us; the launch traced here: 598 us
  Pallas kernels  575 us (96%)
  between operations  14.9 us (2%)
    pallas_call x1, Pallas kernels, fused_update(): pl.pallas_call(functools.partial(update_kernel, classes, steps), grid=(st...  283 us
    pallas_call x1, Pallas kernels, shared_grads(): pl.pallas_call(functools.partial(grad_kernel, classes, groups, steps), gr...  104 us
    pallas_call x1, Pallas kernels, head_pass(): pl.pallas_call(functools.partial(head_kernel, classes, global_rows, spati...  78.3 us
    pallas_call x1, Pallas kernels, front(): pl.pallas_call(functools.partial(front_kernel, spatial, scans, chunks), g...  63 us
    pallas_call x1, Pallas kernels, conv_grad(): pl.pallas_call(functools.partial(conv_grad_kernel, pos_count), grid=(spat...  37.7 us
  transfers between devices with their start and end apart: 2, of which 0 were waited for; matrix products, arithmetic and copies ran while one was open for 0% of the time, Pallas kernels for 67%

profile of v3, /device:TPU:0, one launch (start us, length us, event | category | flops | bytes accessed | tf_op | source)
XLA Modules:
  0.0 598.3 jit_solution(1479770563271684816)
XLA Ops:
  7.2 0.0 all-gather.2.cloned.1.call-start
  7.2 0.0 copy-start
  7.2 63.0 %front.1 = (f32[512,2048]{1,0:T(8,128)}, f32[8,2048]{1,0:T(8,128)}, f32[512,128]{1,0:T(8,128)}, bf16[512,2048]{1,0:T(8,128)(2,1)}, f32[256,2048]{1,0:T(8,128)}, /*index=5*/bf16[49,256,2048]{2,1,0:T(8,128)(2,1)}) custom-call(bf16[49,256,512]{2,1,0:T(8,128)(2,1)} %bitcast.26, bf16[49,256,2048]{2,1,0:T(8,128)(2,1)} %bitcast.25, f32[512,2048]{1,0:T(8,128)} %w_hbm.1, ...), custom_call_target="tpu_custom_call" | custom-call | flops 32883343360 | bytes 102760448 | tf_op jit(solution)/shard_map/front/pallas_call | solution.py:495
  70.3 0.0 all-gather.2.cloned.1.call-update
  70.3 0.2 all-reduce.3.cloned.1.call-start
  70.5 0.0 copy-done
  70.5 0.7 broadcast_in_dim.19.bias
  71.2 0.6 reduce_sum.9
  72.5 78.3 %head_pass.1 = (f32[256,2048]{1,0:T(8,128)}, f32[8,256]{1,0:T(8,128)}, f32[1]{0:T(128)}, f32[22016,128]{1,0:T(8,128)}) custom-call(f32[1]{0:T(128)} %bitcast.1.bsum, s32[256]{0:T(256)} %lab_s.1, f32[21843,2048]{1,0:T(8,128)} %bitcast.w_hbm.tail.refs_0_.refs_1_.refs_2_.refs_3_.refs_4_.refs_5_.refs_6_.refs_7_.refs_8_.w_end, ...), custom_call_target="tpu_custom_call" | custom-call | flops 45808091136 | bytes 178937856 | tf_op jit(solution)/shard_map/head_pass/pallas_call | solution.py:616
  150.8 37.7 %conv_grad.1 = (f32[512,2048]{1,0:T(8,128)}, f32[1,2048]{1,0:T(1,128)}, f32[1,2048]{1,0:T(1,128)}) custom-call(bf16[49,256,512]{2,1,0:T(8,128)(2,1)} %bitcast.27, bf16[49,256,2048]{2,1,0:T(8,128)(2,1)} %get-tuple-element.40.y, f32[256,2048]{1,0:T(8,128)} %get-tuple-element.41.dpool, f32[8,2048]{1,0:T(8,128)} %get-tuple-element.42.stats, ...), custom_call_target="tpu_custom_call" | custom-call | flops 26306674688 | bytes 51380224 | tf_op jit(solution)/shard_map/conv_grad/pallas_call | solution.py:699
  188.5 0.0 all-gather.2.cloned.1.call-done.refs_12_
  188.5 0.0 copy-start.7
  188.5 0.0 copy-start.8
  188.6 104.0 %shared_grads.1 = (f32[2,45,96,2048]{3,2,1,0:T(8,128)}, bf16[2048,2048]{1,0:T(8,128)(2,1)}, f32[15,6,256]{2,1,0:T(8,128)}, f32[8,2048]{1,0:T(8,128)}, f32[8,128]{1,0:T(8,128)}) custom-call(f32[21843,2048]{1,0:T(8,128)} %bitcast.w_hbm.tail.refs_0_.refs_1_.refs_2_.refs_3_.refs_4_.refs_5_.refs_6_.refs_7_.refs_8_.w_end, ...), custom_call_target="tpu_custom_call" | custom-call | flops 72477573120 | bytes 70778880 | tf_op jit(solution)/shard_map/shared_grads/pallas_call | solution.py:215
  292.5 0.9 reshape.33
  293.5 0.0 copy-done.7
  293.5 0.0 copy-done.8
  293.5 1.4 concatenate.3
  294.8 0.0 all-reduce.3.cloned.1.call-update
  294.9 0.0 copy-start.1
  294.9 0.0 copy-start.2
  294.9 0.0 copy-start.3
  294.9 0.0 copy-start.4
  294.9 0.0 copy-start.5
  294.9 0.0 copy-start.6
  294.9 283.2 %fused_update.1 = (f32[21843,2048]{1,0:T(8,128)}, f32[21843,2048]{1,0:T(8,128)}, f32[8,128]{1,0:T(8,128)}) custom-call(f32[8,128]{1,0:T(8,128)} %get-tuple-element.49.rate, f32[21843,2048]{1,0:T(8,128)} %bitcast.w_hbm.tail.refs_0_.refs_1_.refs_2_.refs_3_.refs_4_.refs_5_.refs_6_.refs_7_.refs_8_.w_end, f32[21843,2048]{1,0:T(8,128)} %bitcast.11.v_hbm.v_end, ...), custom_call_target="tpu_custom_call" | custom-call | flops 230854492160 | bytes 715751424 | tf_op jit(solution)/shard_map/fused_update/pallas_call | solution.py:337
  578.1 0.0 all-reduce.3.cloned.1.call-done
  578.2 1.3 slice.24
  579.4 0.0 copy-done.1
  579.4 0.0 copy-done.2
  579.4 1.6 fusion.3
  581.0 0.0 copy-done.3
  581.0 0.0 copy-done.4
  581.0 0.0 copy-done.5
  581.0 0.0 copy-done.6
  581.0 1.5 fusion.5
  582.5 8.9 %conv_update.1 = (f32[512,2048]{1,0:T(8,128)}, f32[512,2048]{1,0:T(8,128)}) custom-call(f32[8,128]{1,0:T(8,128)} %get-tuple-element.53.dep, f32[1]{0:T(128)} %bitcast.19.lr, f32[512,2048]{1,0:T(8,128)} %get-tuple-element.63.g_hbm, f32[512,2048]{1,0:T(8,128)} %w_hbm.1, f32[512,2048]{1,0:T(8,128)} %v_hbm.1), custom_call_target="tpu_custom_call" | custom-call | flops 10485760 | bytes 20971520 | tf_op jit(solution)/shard_map/conv_update/pallas_call | solution.py:398
  (1 shorter events, 0.0 us)
Async XLA Ops:
  7.2 181.3 %all-gather.2.cloned.1.call-start = ((), (), s32[]{:S(2)}) async-start(), calls=%async_computation | async-start | bytes 18874368 | tf_op jit(solution)/shard_map/all_gather | solution.py:727
  7.2 63.3 %copy-start = (f32[21843]{0:T(1024)S(1)}, f32[21843]{0:T(1024)}, u32[]{:S(2)}) copy-start(f32[21843]{0:T(1024)} %param.21) | copy-start | bytes 262120
  70.3 507.8 %all-reduce.3.cloned.1.call-start = ((), (), s32[]{:S(2)}) async-start(), calls=%async_computation.1 | async-start | bytes 8601600 | tf_op jit(solution)/shard_map/psum | solution.py:734
  188.5 104.9 %copy-start.7 = (f32[1,2048]{1,0:T(1,128)S(1)}, f32[1,2048]{1,0:T(1,128)}, u32[]{:S(2)}) copy-start(f32[1,2048]{1,0:T(1,128)} %get-tuple-element.57) | copy-start | bytes 24580
  188.5 104.9 %copy-start.8 = (f32[1,2048]{1,0:T(1,128)S(1)}, f32[1,2048]{1,0:T(1,128)}, u32[]{:S(2)}) copy-start(f32[1,2048]{1,0:T(1,128)} %get-tuple-element.58) | copy-start | bytes 24580
  294.9 284.6 %copy-start.1 = (f32[21843]{0:T(1024)S(1)}, f32[21843]{0:T(1024)}, u32[]{:S(2)}) copy-start(f32[21843]{0:T(1024)} %param.21) | copy-start | bytes 262120
  294.9 284.5 %copy-start.2 = (f32[21843]{0:T(1024)S(1)}, f32[21843]{0:T(1024)}, u32[]{:S(2)}) copy-start(f32[21843]{0:T(1024)} %param.26) | copy-start | bytes 262120
  294.9 286.1 %copy-start.3 = (f32[2048]{0:T(1024)S(1)}, f32[2048]{0:T(1024)}, u32[]{:S(2)}) copy-start(f32[2048]{0:T(1024)} %param.18) | copy-start | bytes 24580
  294.9 286.1 %copy-start.4 = (f32[2048]{0:T(1024)S(1)}, f32[2048]{0:T(1024)}, u32[]{:S(2)}) copy-start(f32[2048]{0:T(1024)} %param.19) | copy-start | bytes 24580
  294.9 286.1 %copy-start.5 = (f32[2048]{0:T(1024)S(1)}, f32[2048]{0:T(1024)}, u32[]{:S(2)}) copy-start(f32[2048]{0:T(1024)} %param.24) | copy-start | bytes 24580
  294.9 286.1 %copy-start.6 = (f32[2048]{0:T(1024)S(1)}, f32[2048]{0:T(1024)}, u32[]{:S(2)}) copy-start(f32[2048]{0:T(1024)} %param.23) | copy-start | bytes 24580
Sparse Core Ops, SparseCore 0:
  70.4 86.9 all-gather.1
  295.0 71.7 all-reduce.2

commit v4 on v3

--- a/solution.py
+++ b/solution.py
@@ -18,7 +18,7 @@
 SLOTS = TILE // BLK
 HAVE = 3
 NORM = 2
-GROUP = 3
+GROUP = 4
 CHUNK = 512
 POS = 7
 WIDTH = 512
@@ -252,6 +252,7 @@
     step = pl.program_id(0)
     a = tiled(rate[0:1, :], CHUNK // LANES)
     cols, feats = p.shape
+    small, decay = a * (1.0 / cols), a * WEIGHT_DECAY
     tall = 2 * TILE
     whole = (classes - (steps - 1) * tall) // SUB * SUB
     done[...] = jnp.zeros_like(done)
@@ -282,9 +283,9 @@
 
     slot = lax.rem(step, DEPTH)
 
-    def apply(rs, cs, g):
+    def apply(rs, cs, g, a):
         w = wbuf[slot, rs, cs]
-        nv = MOMENTUM * vbuf[slot, rs, cs] + a * (g + WEIGHT_DECAY * w)
+        nv = MOMENTUM * vbuf[slot, rs, cs] + a * g + decay * w
         v_out[rs, cs] = nv
         w_out[rs, cs] = w - nv
 
@@ -310,7 +311,7 @@
         z = lax.dot_general(lhs[...], p[cs, :], (((1,), (1,)), ((), ())), preferred_element_type=jnp.float32)
         for t, src in enumerate((even, odd)):
             for i in range(HAVE):
-                apply(aligned(t * TILE + (2 * q + i) % SLOTS * BLK, BLK), cs, src[0, 0, i * BLK:(i + 1) * BLK, cs])
+                apply(aligned(t * TILE + (2 * q + i) % SLOTS * BLK, BLK), cs, src[0, 0, i * BLK:(i + 1) * BLK, cs], a)
         for k, base in enumerate(bases):
             rs = slice(k * BLK, (k + 1) * BLK)
             d = logit_grads(z[rs], bias[aligned(base, BLK), :], rows_in[0:1, cs], rows_in[1:2, cs], step * tall + base, classes)
@@ -318,9 +319,9 @@
 
     for n in range(feats // CHUNK):
         cs = slice(n * CHUNK, (n + 1) * CHUNK)
-        g = jnp.dot(dmat[...], p[:, cs], preferred_element_type=jnp.float32) * (1.0 / cols)
+        g = jnp.dot(dmat[...], p[:, cs], preferred_element_type=jnp.float32)
         for k, base in enumerate(bases):
-            apply(aligned(base, BLK), cs, g[k * BLK:(k + 1) * BLK])
+            apply(aligned(base, BLK), cs, g[k * BLK:(k + 1) * BLK], small)
 
 
 def fused_update(rate, wt, vt, grads, bias, p, rows_in):
@@ -412,7 +413,7 @@
     c_mid = a.shape[-1]
     cols = wc.shape[1]
     pos_count = spatial * a.shape[1]
-    wide = 2 * CHUNK
+    wide = 4 * CHUNK
 
     def fetch(i):
         at = pl.ds(i * POS, POS)

time: 599 us -> 595 us (level)
  no operation moved by 1% of the time
where the time goes in v4:
time: 595 us; the launch traced here: 594 us
  Pallas kernels  571 us (96%)
  between operations  14.9 us (3%)
    pallas_call x1, Pallas kernels, fused_update(): pl.pallas_call(functools.partial(update_kernel, classes, steps), grid=(st...  283 us
    pallas_call x1, Pallas kernels, shared_grads(): pl.pallas_call(functools.partial(grad_kernel, classes, groups, steps), gr...  101 us
    pallas_call x1, Pallas kernels, head_pass(): pl.pallas_call(functools.partial(head_kernel, classes, global_rows, spati...  78.3 us
    pallas_call x1, Pallas kernels, front(): pl.pallas_call(functools.partial(front_kernel, spatial, scans, chunks), g...  62 us
    pallas_call x1, Pallas kernels, conv_grad(): pl.pallas_call(functools.partial(conv_grad_kernel, pos_count), grid=(spat...  37.7 us
  transfers between devices with their start and end apart: 2, of which 0 were waited for; matrix products, arithmetic and copies ran while one was open for 0% of the time, Pallas kernels for 67%

profile of v4, /device:TPU:0, one launch (start us, length us, event | category | flops | bytes accessed | tf_op | source)
XLA Modules:
  0.0 594.0 jit_solution(3559697471590899380)
XLA Ops:
  7.2 0.0 all-gather.2.cloned.1.call-start
  7.2 0.0 copy-start
  7.2 62.0 %front.1 = (f32[512,2048]{1,0:T(8,128)}, f32[8,2048]{1,0:T(8,128)}, f32[512,128]{1,0:T(8,128)}, bf16[512,2048]{1,0:T(8,128)(2,1)}, f32[256,2048]{1,0:T(8,128)}, /*index=5*/bf16[49,256,2048]{2,1,0:T(8,128)(2,1)}) custom-call(bf16[49,256,512]{2,1,0:T(8,128)(2,1)} %bitcast.31, bf16[49,256,2048]{2,1,0:T(8,128)(2,1)} %bitcast.30, f32[512,2048]{1,0:T(8,128)} %w_hbm.1, ...), custom_call_target="tpu_custom_call" | custom-call | flops 32883343360 | bytes 102760448 | tf_op jit(solution)/shard_map/front/pallas_call | solution.py:496
  69.2 0.0 all-gather.2.cloned.1.call-update
  69.3 0.2 all-reduce.3.cloned.1.call-start
  69.5 0.0 copy-done
  69.5 0.7 broadcast_in_dim.19.bias
  70.2 0.6 reduce_sum.9
  71.5 78.3 %head_pass.1 = (f32[256,2048]{1,0:T(8,128)}, f32[8,256]{1,0:T(8,128)}, f32[1]{0:T(128)}, f32[22016,128]{1,0:T(8,128)}) custom-call(f32[1]{0:T(128)} %bitcast.1.bsum, s32[256]{0:T(256)} %lab_s.1, f32[21843,2048]{1,0:T(8,128)} %bitcast.w_hbm.tail.refs_0_.refs_1_.refs_2_.refs_3_.refs_4_.refs_5_.refs_6_.refs_7_.refs_8_.refs_9_.refs_10_.refs_11_.w_end, ...), custom_call_target="tpu_custom_call" | custom-call | flops 45808091136 | bytes 178937856 | tf_op jit(solution)/shard_map/head_pass/pallas_call | solution.py:617
  149.7 37.7 %conv_grad.1 = (f32[512,2048]{1,0:T(8,128)}, f32[1,2048]{1,0:T(1,128)}, f32[1,2048]{1,0:T(1,128)}) custom-call(bf16[49,256,512]{2,1,0:T(8,128)(2,1)} %bitcast.32, bf16[49,256,2048]{2,1,0:T(8,128)(2,1)} %get-tuple-element.40.y, f32[256,2048]{1,0:T(8,128)} %get-tuple-element.41.dpool, f32[8,2048]{1,0:T(8,128)} %get-tuple-element.42.stats, ...), custom_call_target="tpu_custom_call" | custom-call | flops 26306674688 | bytes 51380224 | tf_op jit(solution)/shard_map/conv_grad/pallas_call | solution.py:700
  187.5 0.0 all-gather.2.cloned.1.call-done.refs_16_
  187.5 0.0 copy-start.7
  187.5 0.0 copy-start.8
  187.5 100.6 %shared_grads.1 = (f32[2,44,96,2048]{3,2,1,0:T(8,128)}, bf16[2048,2048]{1,0:T(8,128)(2,1)}, f32[11,8,256]{2,1,0:T(8,128)}, f32[8,2048]{1,0:T(8,128)}, f32[8,128]{1,0:T(8,128)}) custom-call(f32[21843,2048]{1,0:T(8,128)} %bitcast.w_hbm.tail.refs_0_.refs_1_.refs_2_.refs_3_.refs_4_.refs_5_.refs_6_.refs_7_.refs_8_.refs_9_.refs_10_.refs_11_.w_end, ...), custom_call_target="tpu_custom_call" | custom-call | flops 70866960384 | bytes 69206016 | tf_op jit(solution)/shard_map/shared_grads/pallas_call | solution.py:215
  288.2 0.9 copy.25
  289.1 0.0 copy-done.7
  289.1 0.0 copy-done.8
  289.1 1.4 concatenate.3
  290.5 0.0 all-reduce.3.cloned.1.call-update
  290.5 0.0 copy-start.1
  290.5 0.0 copy-start.2
  290.6 0.0 copy-start.3
  290.6 0.0 copy-start.4
  290.6 0.0 copy-start.5
  290.6 0.0 copy-start.6
  290.6 283.3 %fused_update.1 = (f32[21843,2048]{1,0:T(8,128)}, f32[21843,2048]{1,0:T(8,128)}, f32[8,128]{1,0:T(8,128)}) custom-call(f32[8,128]{1,0:T(8,128)} %get-tuple-element.49.rate, f32[21843,2048]{1,0:T(8,128)} %bitcast.w_hbm.tail.refs_0_.refs_1_.refs_2_.refs_3_.refs_4_.refs_5_.refs_6_.refs_7_.refs_8_.refs_9_.refs_10_.refs_11_.w_end, ...), custom_call_target="tpu_custom_call" | custom-call | flops 230854492160 | bytes 715751424 | tf_op jit(solution)/shard_map/fused_update/pallas_call | solution.py:338
  573.9 0.0 all-reduce.3.cloned.1.call-done
  573.9 1.2 slice.24
  575.2 0.0 copy-done.1
  575.2 0.0 copy-done.2
  575.2 1.6 fusion.3
  576.8 0.0 copy-done.3
  576.8 0.0 copy-done.4
  576.8 0.0 copy-done.5
  576.8 0.0 copy-done.6
  576.8 1.5 fusion.5
  578.3 8.9 %conv_update.1 = (f32[512,2048]{1,0:T(8,128)}, f32[512,2048]{1,0:T(8,128)}) custom-call(f32[8,128]{1,0:T(8,128)} %get-tuple-element.53.dep, f32[1]{0:T(128)} %bitcast.22.lr, f32[512,2048]{1,0:T(8,128)} %get-tuple-element.63.g_hbm, f32[512,2048]{1,0:T(8,128)} %w_hbm.1, f32[512,2048]{1,0:T(8,128)} %v_hbm.1), custom_call_target="tpu_custom_call" | custom-call | flops 10485760 | bytes 20971520 | tf_op jit(solution)/shard_map/conv_update/pallas_call | solution.py:399
Async XLA Ops:
  7.2 180.3 %all-gather.2.cloned.1.call-start = ((), (), s32[]{:S(2)}) async-start(), calls=%async_computation | async-start | bytes 18874368 | tf_op jit(solution)/shard_map/all_gather | solution.py:728
  7.2 62.3 %copy-start = (f32[21843]{0:T(1024)S(1)}, f32[21843]{0:T(1024)}, u32[]{:S(2)}) copy-start(f32[21843]{0:T(1024)} %param.21) | copy-start | bytes 262120
  69.3 504.7 %all-reduce.3.cloned.1.call-start = ((), (), s32[]{:S(2)}) async-start(), calls=%async_computation.1 | async-start | bytes 8601600 | tf_op jit(solution)/shard_map/psum | solution.py:735
  187.5 101.6 %copy-start.7 = (f32[1,2048]{1,0:T(1,128)S(1)}, f32[1,2048]{1,0:T(1,128)}, u32[]{:S(2)}) copy-start(f32[1,2048]{1,0:T(1,128)} %get-tuple-element.57) | copy-start | bytes 24580
  187.5 101.6 %copy-start.8 = (f32[1,2048]{1,0:T(1,128)S(1)}, f32[1,2048]{1,0:T(1,128)}, u32[]{:S(2)}) copy-start(f32[1,2048]{1,0:T(1,128)} %get-tuple-element.58) | copy-start | bytes 24580
  290.5 284.6 %copy-start.1 = (f32[21843]{0:T(1024)S(1)}, f32[21843]{0:T(1024)}, u32[]{:S(2)}) copy-start(f32[21843]{0:T(1024)} %param.21) | copy-start | bytes 262120
  290.5 284.6 %copy-start.2 = (f32[21843]{0:T(1024)S(1)}, f32[21843]{0:T(1024)}, u32[]{:S(2)}) copy-start(f32[21843]{0:T(1024)} %param.26) | copy-start | bytes 262120
  290.6 286.2 %copy-start.3 = (f32[2048]{0:T(1024)S(1)}, f32[2048]{0:T(1024)}, u32[]{:S(2)}) copy-start(f32[2048]{0:T(1024)} %param.18) | copy-start | bytes 24580
  290.6 286.2 %copy-start.4 = (f32[2048]{0:T(1024)S(1)}, f32[2048]{0:T(1024)}, u32[]{:S(2)}) copy-start(f32[2048]{0:T(1024)} %param.19) | copy-start | bytes 24580
  290.6 286.2 %copy-start.5 = (f32[2048]{0:T(1024)S(1)}, f32[2048]{0:T(1024)}, u32[]{:S(2)}) copy-start(f32[2048]{0:T(1024)} %param.24) | copy-start | bytes 24580
  290.6 286.2 %copy-start.6 = (f32[2048]{0:T(1024)S(1)}, f32[2048]{0:T(1024)}, u32[]{:S(2)}) copy-start(f32[2048]{0:T(1024)} %param.23) | copy-start | bytes 24580
Sparse Core Ops, SparseCore 0:
  69.4 86.8 all-gather.1
  290.7 72.8 all-reduce.2
